TPU v7x, 128 devices: a whole 4x4x4 slice. The times are simulated.
128 devices in a mesh: ctx: 32 (over x, z, core), head: 4 (over y).
Axes of the slice: x: 4, y: 4, z: 4, core: 2. Of those that a mesh axis runs over, the one named last changes fastest.
Arguments:
- query_nope: bfloat16 [32, 16384], P('ctx', 'head'), may hold values from -15 to 15
- query_rope: bfloat16 [32, 8192], P('ctx', 'head'), may hold values from -8 to 8
- cache_latent: bfloat16 [2048, 128, 512], P('ctx'), may hold values from -6 to 6
- cache_rope: bfloat16 [2048, 8192], P('ctx'), may hold values from -8 to 8
- key_up: bfloat16 [128, 128, 512], P('head'), may hold values from -0.25 to 0.25
- value_up: bfloat16 [128, 512, 128], P('head'), may hold values from -0.25 to 0.25
- lengths: int32 [16], replicated, may hold values from 4096 to 16384, as said below
- block_owner: int32 [2048], P('ctx'), may hold values from -1 to 15, as said below
- block_number: int32 [2048], P('ctx'), may hold values from 0 to 127, as said below
Outputs:
- attended: bfloat16 [32, 16384], P('ctx', 'head')
Inputs may be any that keep to these rules, and one draw needn't show every extreme that they name: `lengths`: at least one sequence has exactly 16384 positions. A slot with block_owner -1 holds nothing. Sequence b owns exactly ceil(lengths[b] / 128) slots. The slots of sequence b carry block_number 0 to ceil(lengths[b] / 128) - 1, each once; empty slots carry 0.
All inputs are finite; a program needn't handle non-finite values.
Results may differ from a plain program's by a relative error of at most 0.023.
Values may be sent and summed in bfloat16 or wider, within the bound.
A program may use at most 128 MiB of HBM per device.

v0:
```python
import math

import jax
import jax.numpy as jnp
from jax import lax
from jax.sharding import PartitionSpec as P

score_scale = 192.0 ** (-0.5) * (1.0 + 0.1 * math.log(40.0)) ** 2
floor_value = -1e30


def sent_together(arrays, axis, dim, along):
    both = jnp.concatenate(arrays, axis=along)
    whole, at, finished = (lax.all_gather(both, axis, axis=dim, tiled=True), 0, [])
    for a in arrays:
        finished.append(lax.slice_in_dim(whole, at, at + a.shape[along], axis=along))
        at += a.shape[along]
    return tuple(finished)


def copy_for_each(value, axis):
    copies = jnp.broadcast_to(value, (lax.axis_size(axis), *value.shape))
    return lax.all_to_all(copies, axis, split_axis=0, concat_axis=0, tiled=True)


def of_everyone(value, axis):
    return copy_for_each(value, axis).max(axis=0)


def split_up(value, dim, size):
    before, after = (value.shape[:dim], value.shape[dim + 1 :])
    return jnp.moveaxis(value.reshape(*before, size, -1, *after), dim, 0)


def summed_on_arrival(value, axis, dim):
    parts = split_up(value, dim, lax.axis_size(axis))
    arrived = lax.all_to_all(parts, axis, split_axis=0, concat_axis=0, tiled=True)
    return arrived.astype(jnp.float32).sum(axis=0)


def side_by_side(arrays, axis, dim, along):
    widths = [math.prod(a.shape[along:]) for a in arrays]
    both = jnp.concatenate(
        [a.reshape(*a.shape[:along], w) for a, w in zip(arrays, widths)], axis=along
    )
    whole = summed_on_arrival(both, axis, dim)
    parts = jnp.split(whole, [sum(widths[:k]) for k in range(1, len(widths))], axis=along)
    return tuple((b.reshape(*whole.shape[:along], *a.shape[along:]) for a, b in zip(arrays, parts)))


def per_device(
    query_nope,
    query_rope,
    cache_latent,
    cache_rope,
    key_up,
    value_up,
    lengths,
    block_owner,
    block_number,
):
    ctx_count = lax.axis_size("ctx")
    row_part = query_nope.shape[0]
    head_part = key_up.shape[0]
    nope_width = key_up.shape[1]
    latent_width = key_up.shape[2]
    value_width = value_up.shape[2]
    rope_width = query_rope.shape[1] // head_part
    rows_all = row_part * ctx_count
    seq_count = lengths.shape[0]
    new_tokens = rows_all // seq_count
    block_count = cache_latent.shape[0]
    block_width = cache_latent.shape[1]
    query_count = rows_all * head_part
    own_query = jnp.einsum(
        "rhn,hnc->rhc",
        query_nope.reshape(row_part, head_part, nope_width),
        key_up,
        preferred_element_type=jnp.float32,
    ).astype(jnp.bfloat16)
    own_rope = query_rope.reshape(row_part, head_part, rope_width)
    full_query, full_rope = sent_together((own_query, own_rope), "ctx", 0, 2)
    flat_query = full_query.reshape(query_count, latent_width)
    flat_rope = full_rope.reshape(query_count, rope_width)
    per_step = math.gcd(block_count, 32)
    turn_count = block_count // per_step
    key_count = per_step * block_width
    latent_sets = cache_latent.reshape(turn_count, key_count, latent_width)
    rope_sets = cache_rope.reshape(turn_count, key_count, rope_width)
    owner_sets = block_owner.reshape(turn_count, per_step)
    number_sets = block_number.reshape(turn_count, per_step)
    row_ids = jnp.arange(rows_all, dtype=jnp.int32)
    row_seq = row_ids // new_tokens
    row_limit = lengths[row_seq] - (new_tokens - 1 - row_ids % new_tokens)
    slot_ids = jnp.arange(block_width, dtype=jnp.int32)

    def attend(running, blockset):
        row_top, row_total, row_accum = running
        key_latent, rope_keys, owners, numbers = blockset
        logits = jnp.einsum("qc,kc->qk", flat_query, key_latent, preferred_element_type=jnp.float32)
        logits = logits + jnp.einsum(
            "qd,kd->qk", flat_rope, rope_keys, preferred_element_type=jnp.float32
        )
        logits = logits * score_scale
        key_owner = jnp.repeat(owners, block_width)
        key_position = (numbers[:, None] * block_width + slot_ids[None, :]).reshape(key_count)
        visible = (key_owner[None, :] == row_seq[:, None]) & (
            key_position[None, :] < row_limit[:, None]
        )
        visible = jnp.broadcast_to(visible[:, None, :], (rows_all, head_part, key_count)).reshape(
            query_count, key_count
        )
        logits = jnp.where(visible, logits, floor_value)
        new_top = jnp.maximum(row_top, jnp.max(logits, axis=1))
        weight = jnp.where(visible, jnp.exp(logits - new_top[:, None]), 0.0)
        part_total = jnp.sum(weight, axis=1)
        part_accum = jnp.dot(
            weight.astype(jnp.bfloat16), key_latent, preferred_element_type=jnp.float32
        )
        shrink = jnp.exp(row_top - new_top)
        return (new_top, row_total * shrink + part_total, row_accum * shrink[:, None] + part_accum)

    def advance(running, blockset):
        result = attend(running, blockset)
        return (result, None)

    starting = (
        jnp.full((query_count,), floor_value, jnp.float32),
        jnp.zeros((query_count,), jnp.float32),
        jnp.zeros((query_count, latent_width), jnp.float32),
    )
    running, unused = lax.scan(advance, starting, (latent_sets, rope_sets, owner_sets, number_sets))
    row_top = running[0].reshape(rows_all, head_part)
    row_total = running[1].reshape(rows_all, head_part)
    row_accum = running[2].reshape(rows_all, head_part, latent_width)
    value_real = value_up.astype(jnp.float32)
    global_top = of_everyone(row_top, "ctx")
    factor = jnp.exp(row_top - global_top)
    scaled_accum = jnp.einsum("rhc,hcv->rhv", row_accum * factor[:, :, None], value_real).reshape(
        ctx_count, row_part, head_part, value_width
    )
    scaled_total = (row_total * factor).reshape(ctx_count, row_part, head_part)
    summed = side_by_side(
        (scaled_accum.astype(jnp.bfloat16), scaled_total.astype(jnp.bfloat16)), "ctx", 0, 3
    )
    attended = summed[0][0] / summed[1][0][:, :, None]
    return attended.astype(jnp.bfloat16).reshape(row_part, head_part * value_width)


def solution(mesh):
    return jax.shard_map(
        per_device,
        mesh=mesh,
        in_specs=(
            P("ctx", "head"),
            P("ctx", "head"),
            P("ctx", None, None),
            P("ctx", None),
            P("head", None, None),
            P("head", None, None),
            P(),
            P("ctx"),
            P("ctx"),
        ),
        out_specs=P("ctx", "head"),
        check_vma=False,
    )
```

profile of v0, /device:TPU:1, one launch (start us, length us, event | category | flops | bytes accessed | tf_op | source)
XLA Modules:
  0.0 211.1 jit_solution(8288801655035344976)
XLA Ops:
  6.6 0.6 copy-done
  7.3 2.8 %fusion.39 = bf16[32,1,512]{2,1,0:T(2,128)(2,1)S(1)} fusion(bf16[32,128,512]{2,1,0:T(8,128)(2,1)} %param.15, bf16[1,4096]{1,0:T(2,128)(2,1)S(1)} %copy-done), kind=kOutput, calls=%fused_computation.55 | convolution fusion | flops 4194304 | bytes 4235264 | tf_op jit(solution)/shard_map/rhn,hnc->rhc/dot_general | solution.py:75
  10.2 0.6 pad_maximum_fusion
  10.9 2.3 %reshape.257 = bf16[2,4096,64]{2,1,0:T(8,128)(2,1)S(1)} reshape(bf16[64,8192]{1,0:T(8,128)(2,1)S(1)} %copy-done.5) | data formatting | bytes 2097152 | tf_op jit(solution)/shard_map/reshape | solution.py:89
  13.4 0.7 gather_fusion
  14.1 43.3 %all-gather.2.cloned.1.call-done = bf16[32,32,576]{2,1,0:T(8,128)(2,1)} async-done(((bf16[1,32,576]{2,1,0:T(8,128)(2,1)}), bf16[32,32,576]{2,1,0:T(8,128)(2,1)}) %all-gather.2.cloned.1.call-update) | async-done | bytes 1179664 | tf_op jit(solution)/shard_map/all_gather | solution.py:14
  57.4 1.3 slice.10
  58.7 1.0 slice.11
  59.7 108.0 %while.15 = (s32[]{:T(128)}, f32[1024]{0:T(1024)S(1)}, f32[1024]{0:T(1024)S(1)}, f32[1024,512]{1,0:T(8,128)}, s32[2,32]{1,0:T(2,128)S(1)}, /*index=5*/s32[2,32]{...) while((s32[]{:T(128)}, f32[1024]{0:T(1024)S(1)}, ...), condition=%wide.region_3.4_spmd.clone, body=%wide.region_0.3_spmd.clone.sunk | while | flops 9170724864 | bytes 174720848 | solution.py:132
  59.9 0.2 compare_and_fusion.2
  60.0 1.1 broadcast_in_dim.60
  61.1 7.7 %copy.69 = pred[1024,4096]{0,1:T(32,128)(4,1)S(1)} copy(pred[1024,4096]{1,0:T(32,128)(4,1)S(1)} %bitcast.79) | data formatting | bytes 8388608 | tf_op jit(solution)/shard_map/while/body/eval_jaxpr/reshape | solution.py:110
  68.9 8.2 %fusion.68 = f32[4096,1024]{1,0:T(8,128)} fusion(bf16[1024,512]{1,0:T(8,128)(2,1)S(1)} %get-tuple-element.258, bf16[2,4096,512]{2,1,0:T(8,128)(2,1)S(1)} %copy-done.7, s32[]{:T(128)} %get-tuple-element.237), kind=kOutput, calls=%fused_computation.11.clone.1 | convolution fusion | flops 4294967296 | bytes 22020100 | tf_op jit(solution)/shard_map/while/body/eval_jaxpr/qc,kc->qk/dot_general | solution.py:100
  77.2 11.0 %fusion.69 = (f32[1024]{0:T(1024)S(1)}, f32[1024,4096]{0,1:T(8,128)}) fusion(pred[1024,4096]{0,1:T(32,128)(4,1)S(1)} %copy.69, f32[4096,1024]{1,0:T(8,128)} %fusion.68, bf16[1024,64]{1,0:T(8,128)(2,1)S(1)} %get-tuple-element.260, bf16[2,4096,64]{2,1,0:T(8,128)(2,1)S(1)} %get-tuple-element.259, s32[]{:T(128)} %get-tuple-element.237), kind=kOutput, calls=%fused_computation.69.clone.1 | convolution fusion | flops 553647104 | bytes 39063556 | tf_op jit(solution)/shard_map/while/body/eval_jaxpr/qd,kd->qk/dot_general | solution.py:101
  88.1 11.2 %fusion.70 = f32[1024]{0:T(1024)S(1)} fusion(pred[1024,4096]{0,1:T(32,128)(4,1)} %copy-done.2, f32[1024,4096]{0,1:T(8,128)} %get-tuple-element.221, f32[1024]{0:T(1024)S(1)} %select_maximum_fusion.2), kind=kLoop, calls=%fused_computation.6.clone.1 | loop fusion | flops 12581888 | bytes 20979712 | tf_op jit(solution)/shard_map/while/body/eval_jaxpr/reduce_sum | solution.py:116
  99.3 14.1 %fusion.72 = f32[1024,512]{1,0:T(8,128)} fusion(f32[1024,512]{1,0:T(8,128)} %get-tuple-element.240, bf16[2,4096,512]{2,1,0:T(8,128)(2,1)} %get-tuple-element.257, s32[]{:T(128)} %get-tuple-element.237, pred[1024,4096]{0,1:T(32,128)(4,1)} %copy-done.2, f32[1024,4096]{0,1:T(8,128)} %get-tuple-element.221, f32[1024]{0:T(1024)S(1)} %select_maximum_fusion.2, ...), kind=kOutput, calls=%fused_computation.16.clone.1 | convolution fusion | flops 4309123072 | bytes 29368832 | tf_op jit(solution)/shard_map/while/body/eval_jaxpr/dot_general | solution.py:117
  113.7 1.1 broadcast_in_dim.60
  114.8 7.7 %copy.69 = pred[1024,4096]{0,1:T(32,128)(4,1)S(1)} copy(pred[1024,4096]{1,0:T(32,128)(4,1)S(1)} %bitcast.79) | data formatting | bytes 8388608 | tf_op jit(solution)/shard_map/while/body/eval_jaxpr/reshape | solution.py:110
  122.6 8.2 %fusion.68 = f32[4096,1024]{1,0:T(8,128)} fusion(bf16[1024,512]{1,0:T(8,128)(2,1)S(1)} %get-tuple-element.258, bf16[2,4096,512]{2,1,0:T(8,128)(2,1)S(1)} %copy-done.7, s32[]{:T(128)} %get-tuple-element.237), kind=kOutput, calls=%fused_computation.11.clone.1 | convolution fusion | flops 4294967296 | bytes 22020100 | tf_op jit(solution)/shard_map/while/body/eval_jaxpr/qc,kc->qk/dot_general | solution.py:100
  130.9 11.0 %fusion.69 = (f32[1024]{0:T(1024)S(1)}, f32[1024,4096]{0,1:T(8,128)}) fusion(pred[1024,4096]{0,1:T(32,128)(4,1)S(1)} %copy.69, f32[4096,1024]{1,0:T(8,128)} %fusion.68, bf16[1024,64]{1,0:T(8,128)(2,1)S(1)} %get-tuple-element.260, bf16[2,4096,64]{2,1,0:T(8,128)(2,1)S(1)} %get-tuple-element.259, s32[]{:T(128)} %get-tuple-element.237), kind=kOutput, calls=%fused_computation.69.clone.1 | convolution fusion | flops 553647104 | bytes 39063556 | tf_op jit(solution)/shard_map/while/body/eval_jaxpr/qd,kd->qk/dot_general | solution.py:101
  141.8 11.2 %fusion.70 = f32[1024]{0:T(1024)S(1)} fusion(pred[1024,4096]{0,1:T(32,128)(4,1)} %copy-done.2, f32[1024,4096]{0,1:T(8,128)} %get-tuple-element.221, f32[1024]{0:T(1024)S(1)} %select_maximum_fusion.2), kind=kLoop, calls=%fused_computation.6.clone.1 | loop fusion | flops 12581888 | bytes 20979712 | tf_op jit(solution)/shard_map/while/body/eval_jaxpr/reduce_sum | solution.py:116
  153.0 14.7 %fusion.72 = f32[1024,512]{1,0:T(8,128)} fusion(f32[1024,512]{1,0:T(8,128)} %get-tuple-element.240, bf16[2,4096,512]{2,1,0:T(8,128)(2,1)} %get-tuple-element.257, s32[]{:T(128)} %get-tuple-element.237, pred[1024,4096]{0,1:T(32,128)(4,1)} %copy-done.2, f32[1024,4096]{0,1:T(8,128)} %get-tuple-element.221, f32[1024]{0:T(1024)S(1)} %select_maximum_fusion.2, ...), kind=kOutput, calls=%fused_computation.16.clone.1 | convolution fusion | flops 4309123072 | bytes 29368832 | tf_op jit(solution)/shard_map/while/body/eval_jaxpr/dot_general | solution.py:117
  167.8 0.9 reshape.278
  168.7 5.3 %all-to-all-start = ((f32[32,1,1024]{2,1,0:T(1,128)}), f32[32,1,1024]{2,1,0:T(1,128)S(1)}, u32[]{:S(2)}, u32[]{:S(2)}) async-start(f32[32,1,1024]{2,1,0:T(1,128)} %reshape.278), calls=%async_computation | async-start | bytes 262144 | tf_op jit(solution)/shard_map/all_to_all | solution.py:23
  174.2 7.5 %all-to-all-done = f32[32,1,1024]{2,1,0:T(1,128)S(1)} async-done(((f32[32,1,1024]{2,1,0:T(1,128)}), f32[32,1,1024]{2,1,0:T(1,128)S(1)}, u32[]{:S(2)}, u32[]{:S(2)}) %all-to-all-start) | async-done | bytes 131104 | tf_op jit(solution)/shard_map/all_to_all | solution.py:23
  181.7 0.5 broadcast.165
  182.2 0.9 reduce.4
  183.5 0.5 copy.52
  184.1 3.6 %fusion.33 = bf16[32,1,32,128]{3,0,2,1:T(8,128)(2,1)S(1)} fusion(bf16[32,512,128]{2,1,0:T(8,128)(2,1)} %param.16, f32[32,32,512]{2,1,0:T(8,128)S(1)} %bitcast.81, f32[32,32]{0,1:T(8,128)S(1)} %copy.50), kind=kOutput, calls=%fused_computation.43 | convolution fusion | flops 134873088 | bytes 6557696 | tf_op jit(solution)/shard_map/rhc,hcv->rhv/dot_general | solution.py:139
  187.8 0.3 copy.53
  188.1 15.2 %all_to_all.10 = bf16[32,1,1,32,129]{4,3,2,1,0:T(8,128)(2,1)S(1)} all-to-all(bf16[32,1,1,32,129]{4,3,2,1,0:T(8,128)(2,1)S(1)} %copy.53), channel_id=1, replica_groups=mesh['ctx'=32,'head'=4] {'ctx'}, dimensions={0} | all-to-all | bytes 528384 | tf_op jit(solution)/shard_map/all_to_all | solution.py:37
  203.6 0.6 divide_convert_fusion
  (65 shorter events, 1.9 us)
Async XLA Ops:
  6.5 0.7 copy-start
  6.5 3.6 %copy-start.6 = (bf16[1,2048]{1,0:T(2,128)(2,1)S(1)}, bf16[1,2048]{1,0:T(2,128)(2,1)}, u32[]{:S(2)}) copy-start(bf16[1,2048]{1,0:T(2,128)(2,1)} %param.12) | copy-start | bytes 12292
  6.5 4.4 %copy-start.5 = (bf16[64,8192]{1,0:T(8,128)(2,1)S(1)}, bf16[64,8192]{1,0:T(8,128)(2,1)}, u32[]{:S(2)}) copy-start(bf16[64,8192]{1,0:T(8,128)(2,1)} %param.14) | copy-start | bytes 3145732
  6.5 6.7 %copy-start.8 = (s32[64]{0:T(128)S(1)}, s32[64]{0:T(128)}, u32[]{:S(2)}) copy-start(s32[64]{0:T(128)} %param.18) | copy-start | bytes 772
  6.5 6.8 %copy-start.9 = (s32[64]{0:T(128)S(1)}, s32[64]{0:T(128)}, u32[]{:S(2)}) copy-start(s32[64]{0:T(128)} %param.19) | copy-start | bytes 772
  6.5 6.9 %copy-start.3 = (s32[16]{0:T(128)S(1)}, s32[16]{0:T(128)}, u32[]{:S(2)}) copy-start(s32[16]{0:T(128)} %param.17) | copy-start | bytes 196
  6.6 50.8 %all-gather.2.cloned.1.call-start = ((), (), s32[]{:S(2)}) async-start(), calls=%async_computation.2 | async-start | bytes 1351680 | tf_op jit(solution)/shard_map/all_gather | solution.py:14
  61.1 7.8 %copy-start.7 = (bf16[2,4096,512]{2,1,0:T(8,128)(2,1)S(1)}, bf16[2,4096,512]{2,1,0:T(8,128)(2,1)}, u32[]{:S(2)}) copy-start(bf16[2,4096,512]{2,1,0:T(8,128)(2,1)} %get-tuple-element.257) | copy-start | bytes 25165828 | tf_op jit(solution)/shard_map/while
  68.9 8.3 %copy-start.2 = (pred[1024,4096]{0,1:T(32,128)(4,1)}, pred[1024,4096]{0,1:T(32,128)(4,1)S(1)}, u32[]{:S(2)}) copy-start(pred[1024,4096]{0,1:T(32,128)(4,1)S(1)} %copy.69) | copy-start | bytes 12582916 | tf_op jit(solution)/shard_map/while
  114.8 7.8 %copy-start.7 = (bf16[2,4096,512]{2,1,0:T(8,128)(2,1)S(1)}, bf16[2,4096,512]{2,1,0:T(8,128)(2,1)}, u32[]{:S(2)}) copy-start(bf16[2,4096,512]{2,1,0:T(8,128)(2,1)} %get-tuple-element.257) | copy-start | bytes 25165828 | tf_op jit(solution)/shard_map/while
  122.6 8.3 %copy-start.2 = (pred[1024,4096]{0,1:T(32,128)(4,1)}, pred[1024,4096]{0,1:T(32,128)(4,1)S(1)}, u32[]{:S(2)}) copy-start(pred[1024,4096]{0,1:T(32,128)(4,1)S(1)} %copy.69) | copy-start | bytes 12582916 | tf_op jit(solution)/shard_map/while
  167.7 16.4 %copy-start.4 = (f32[1024,512]{1,0:T(8,128)S(1)}, f32[1024,512]{1,0:T(8,128)}, u32[]{:S(2)}) copy-start(f32[1024,512]{1,0:T(8,128)} %get-tuple-element.74) | copy-start | bytes 6291460
  168.7 13.0 %all-to-all-start = ((f32[32,1,1024]{2,1,0:T(1,128)}), f32[32,1,1024]{2,1,0:T(1,128)S(1)}, u32[]{:S(2)}, u32[]{:S(2)}) async-start(f32[32,1,1024]{2,1,0:T(1,128)} %reshape.278), calls=%async_computation | async-start | bytes 262144 | tf_op jit(solution)/shard_map/all_to_all | solution.py:23
  184.1 20.2 %copy-start.1 = (bf16[1,4096]{1,0:T(2,128)(2,1)S(1)}, bf16[1,4096]{1,0:T(2,128)(2,1)}, u32[]{:S(2)}) copy-start(bf16[1,4096]{1,0:T(2,128)(2,1)} %param.11) | copy-start | bytes 24580
Sparse Core Ops, SparseCore 0:
  11.0 46.3 all-gather.1
where the time goes:
time: 211 us
  matrix products  73.6 us (35%)
  waiting for transfers between devices  50.8 us (24%)
  local copies, waits for them, and re-layouts  26.9 us (13%)
  other arithmetic  25.5 us (12%)
  blocking collectives  15.2 us (7%)
  between operations  13.6 us (6%)
  starting transfers between devices  5.34 us (3%)
    all_gather x1, waiting for transfers between devices, sent_together(): lax.all_gather(both, axis, axis=dim, tiled=True)  43.3 us
    dot_general x2, matrix products, attend(): jnp.dot(weight.astype(jnp.bfloat16), key_latent, preferred_element_type=j...  28.7 us
    reduce_sum x2, other arithmetic, attend(): part_total = jnp.sum(weight, axis=1)  22.4 us
    dot_general x2, matrix products, attend(): jnp.einsum('qd,kd->qk', flat_rope, rope_keys, preferred_element_type=jnp....  21.9 us
    dot_general x2, matrix products, attend(): jnp.einsum('qc,kc->qk', flat_query, key_latent, preferred_element_type=jn...  16.5 us
    reshape x2, local copies, waits for them, and re-layouts, attend(): jnp.broadcast_to(visible[:, None, :], (rows_all, head_part, key_count))  15.5 us
    all_to_all x1, blocking collectives, summed_on_arrival(): lax.all_to_all(parts, axis, split_axis=0, concat_axis=0, tiled=True)  15.2 us
    all_to_all x1, waiting for transfers between devices, copy_for_each(): return lax.all_to_all(copies, axis, split_axis=0, concat_axis=0, tiled=True)  7.53 us
  transfers between devices with their start and end apart: 2, of which 2 were waited for; matrix products, arithmetic and copies ran while one was open for 2% of the time, Pallas kernels for 0%

commit v1 on v0

v1 whole, which is shorter than its diff:
```python
import functools
import math

import jax
import jax.numpy as jnp
from jax import lax
from jax.experimental import pallas as pl
from jax.experimental.pallas import tpu as pltpu
from jax.sharding import PartitionSpec as P

MESH = pl.DeviceIdType.MESH
score_scale = 192.0 ** (-0.5) * (1.0 + 0.1 * math.log(40.0)) ** 2
floor_value = -1e30
f32 = jnp.float32
bf16 = jnp.bfloat16
LANES = 128
CORES = 2


def pad8(n):
    return (n + 7) // 8 * 8


class Sizes:
    def __init__(self, ctx, rows, heads, nope, rope, latent, value, slots, block, seqs):
        self.ctx, self.rows, self.heads = ctx, rows, heads
        self.nope, self.rope, self.latent, self.value = nope, rope, latent, value
        self.slots, self.block, self.seqs = slots, block, seqs
        self.chips = ctx // CORES
        self.tokens = rows // seqs
        self.pairs = heads // 2
        self.queries = self.tokens * heads
        self.chunks = latent // LANES
        self.block_rows = heads + self.pairs
        self.gather_stride = pad8(self.block_rows) + 8
        self.head_stride = heads + 8
        self.key_stride = block + 8


def kernel(
    z,
    qn_hbm, qr_hbm, lat_hbm, kr_hbm, ku_hbm, vu_hbm, len_hbm, own_hbm, ownrow_hbm, num_hbm,
    out_ref,
    qn, qr, lat, kr, ku, vu, len_s, own_s, num_s, own_v, meta_v, meta_s,
    gath, qstage, gathf, rk, qlt, ql, qro, sc, mpre, mtop, lpre, opre, ot, yt,
    send, recv, stat, statr, acc,
    load_sem, meta_sem, gs_sem, gr_sem, fs_sem, fr_sem, es_sem, er_sem, ss_sem, sr_sem,
):
    me = lax.axis_index("ctx")
    chip = me // CORES
    core = me - chip * CORES
    partner = chip * CORES + (1 - core)

    def peer_chip(i):
        return lax.rem(chip + i, z.chips)

    def source_chip(i):
        return lax.rem(chip - i + z.chips, z.chips)

    loads = [
        pltpu.make_async_copy(s, d, load_sem.at[k])
        for k, (s, d) in enumerate(
            [(qn_hbm, qn), (qr_hbm, qr), (ownrow_hbm, own_v), (len_hbm, len_s), (own_hbm, own_s),
             (num_hbm, num_s), (kr_hbm, kr), (ku_hbm, ku), (lat_hbm, lat), (vu_hbm, vu)]
        )
    ]
    ld_qn, ld_qr, ld_ownv, ld_len, ld_own, ld_num, ld_kr, ld_ku, ld_lat, ld_vu = loads
    for c in loads:
        c.start()

    barrier = pltpu.get_barrier_semaphore()
    for i in range(z.chips):
        for q in range(CORES):
            target = peer_chip(i) * CORES + lax.rem(core + q, CORES)
            if i == 0 and q == 0:
                continue
            pl.semaphore_signal(barrier, inc=1, device_id={"ctx": target}, device_id_type=MESH)

    ld_qn.wait()
    ld_qr.wait()
    for h in range(z.heads):
        qstage[h : h + 1, :] = qn[:, h * LANES : (h + 1) * LANES].astype(f32)
    for h in range(z.pairs):
        qstage[z.heads + h : z.heads + h + 1, :] = qr[:, h * LANES : (h + 1) * LANES].astype(f32)
    gath[me] = qstage[...].astype(bf16)

    pl.semaphore_wait(barrier, z.ctx - 1)

    def gather_copy(i, row):
        return pltpu.make_async_remote_copy(
            src_ref=gath.at[row], dst_ref=gath.at[row], send_sem=gs_sem.at[i], recv_sem=gr_sem.at[i],
            device_id={"ctx": peer_chip(i) * CORES + core}, device_id_type=MESH,
        )

    def forward_copy(i, row):
        return pltpu.make_async_remote_copy(
            src_ref=gath.at[row], dst_ref=gath.at[row], send_sem=fs_sem.at[i], recv_sem=fr_sem.at[i],
            device_id={"ctx": partner}, device_id_type=MESH,
        )

    order = list(range(1, z.chips))
    for i in order:
        gather_copy(i, me).start()
    forward_copy(0, me).start()

    ld_ownv.wait()
    n = z.slots
    own_row = jnp.broadcast_to(own_v[...], (n, n))
    row_i = lax.broadcasted_iota(jnp.int32, (n, n), 0)
    col_i = lax.broadcasted_iota(jnp.int32, (n, n), 1)
    key_row = own_row * n + col_i
    key_col = jnp.sum(jnp.where(row_i == col_i, key_row, 0), axis=1, keepdims=True)
    rank_col = jnp.sum(jnp.where(key_row < key_col, 1, 0), axis=1, keepdims=True)
    perm = jnp.sum(jnp.where(rank_col == col_i, row_i, 0), axis=0, keepdims=True)
    ends = jnp.sum(jnp.where(key_col < (col_i + 1) * n, 1, 0), axis=0, keepdims=True)
    meta_v[0:1, 0:n] = perm
    meta_v[1:2, 0:n] = ends
    meta_copy = pltpu.make_async_copy(meta_v, meta_s, meta_sem)
    meta_copy.start()

    ld_kr.wait()

    rkf = rk.reshape(n * z.key_stride, LANES)

    def spread_keys(j, carry):
        part = kr[:, pl.ds(pl.multiple_of(j * LANES, LANES), LANES)].astype(f32)
        rkf[pl.ds(2 * j, n, stride=z.key_stride), :] = part
        rkf[pl.ds(2 * j + 1, n, stride=z.key_stride), :] = pltpu.roll(part, z.rope, 1)
        return carry

    lax.fori_loop(0, z.block * z.rope // LANES, spread_keys, 0, unroll=2)

    for i in order:
        gather_copy(i, source_chip(i) * CORES + core).wait_recv()
        forward_copy(i, source_chip(i) * CORES + core).start()
    for i in range(z.chips):
        forward_copy(i, source_chip(i) * CORES + (1 - core)).wait_recv()

    def to_rows(r, carry):
        gathf[pl.ds(pl.multiple_of(r * z.gather_stride, 8), z.block_rows), :] = gath[r].astype(f32)
        return carry

    lax.fori_loop(0, z.rows, to_rows, 0, unroll=2)

    ld_ku.wait()
    span = z.rows * z.head_stride

    def absorb(i, carry):
        for e in range(2):
            h = 2 * i + e
            x = gathf[pl.ds(h, z.rows, stride=z.gather_stride), :].astype(bf16)
            y = jnp.dot(x, ku[h], preferred_element_type=f32)
            place = e * z.pairs + i
            for c in range(z.chunks):
                qlt[pl.ds(c * span + place, z.rows, stride=z.head_stride), :] = y[:, c * LANES : (c + 1) * LANES]
        return carry

    lax.fori_loop(0, z.pairs, absorb, 0, unroll=2)

    lane_p = lax.broadcasted_iota(jnp.int32, (z.pairs, LANES), 1)

    def queries(b, carry):
        for j in range(z.tokens):
            r = b * z.tokens + j
            for c in range(z.chunks):
                start = pl.multiple_of(c * span + r * z.head_stride, 8)
                ql[b, j * z.heads : (j + 1) * z.heads, c * LANES : (c + 1) * LANES] = qlt[
                    pl.ds(start, z.heads), :
                ].astype(bf16)
            both = gathf[pl.ds(pl.multiple_of(r * z.gather_stride + z.heads, 8), z.pairs), :]
            qro[b, j * z.heads : j * z.heads + z.pairs, :] = jnp.where(lane_p < z.rope, both, 0.0)
            other = pltpu.roll(both, z.rope, 1)
            qro[b, j * z.heads + z.pairs : (j + 1) * z.heads, :] = jnp.where(lane_p < z.rope, other, 0.0)
        return carry

    lax.fori_loop(0, z.seqs, queries, 0)

    for c in (ld_len, ld_own, ld_num, ld_lat):
        c.wait()
    meta_copy.wait()
    token = lax.broadcasted_iota(jnp.int32, (z.queries, z.block), 0) // z.heads
    place = lax.broadcasted_iota(jnp.int32, (z.queries, z.block), 1) - token
    contract_last = (((1,), (1,)), ((), ()))

    def score(j, carry):
        top, before = carry
        p = meta_s[0, j]
        o = own_s[p]
        b = jnp.maximum(o, 0)
        limit = jnp.where(o >= 0, len_s[b] - (z.tokens - 1) - num_s[p] * z.block, -z.tokens)
        s = lax.dot_general(ql[b], lat[p], contract_last, preferred_element_type=f32)
        keys = rk[p, 0 : z.block, :]
        s = s + lax.dot_general(qro[b], keys, contract_last, preferred_element_type=f32)
        s = jnp.where(place < limit, s * score_scale, floor_value)
        sc[j] = s
        top = jnp.maximum(jnp.where(o == before, top, floor_value), s)
        mpre[j] = top
        return top, o

    lax.fori_loop(
        0, n, score, (jnp.full((z.queries, z.block), floor_value, f32), jnp.int32(-2)), unroll=4
    )

    lane_q = lax.broadcasted_iota(jnp.int32, (z.queries, LANES), 1)

    def segment(b):
        end = meta_s[1, b]
        return jnp.maximum(end - 1, 0), end

    def has_any(b):
        last, end = segment(b)
        return (end > 0) & (own_s[meta_s[0, last]] == b)

    def tops(b, stats):
        last, _ = segment(b)
        m = jnp.max(mpre[last], axis=1, keepdims=True)
        m = jnp.where(has_any(b), m, floor_value)
        mtop[b] = jnp.broadcast_to(m, (z.queries, z.block))
        return jnp.where(lane_q == b, m, stats)

    stats = lax.fori_loop(0, z.seqs, tops, jnp.zeros((z.queries, LANES), f32), unroll=2)

    def weigh(j, carry):
        total, before = carry
        p = meta_s[0, j]
        o = own_s[p]
        b = jnp.maximum(o, 0)
        w = jnp.exp(sc[j] - mtop[b])
        keep = o == before
        total = jnp.where(keep, total, 0.0) + w
        lpre[j] = total
        old = opre[jnp.maximum(j - 1, 0)]
        opre[j] = jnp.where(keep, old, 0.0) + jnp.dot(w.astype(bf16), lat[p], preferred_element_type=f32)
        return total, o

    lax.fori_loop(0, n, weigh, (jnp.zeros((z.queries, z.block), f32), jnp.int32(-2)), unroll=4)

    def finish(b, stats):
        last, _ = segment(b)
        t = jnp.sum(lpre[last], axis=1, keepdims=True)
        for j in range(z.tokens):
            r = b * z.tokens + j
            for c in range(z.chunks):
                start = pl.multiple_of(c * span + r * z.head_stride, 8)
                ot[pl.ds(start, z.heads), :] = opre[
                    last, j * z.heads : (j + 1) * z.heads, c * LANES : (c + 1) * LANES
                ]
        return jnp.where(lane_q == z.seqs + b, t, stats)

    stats = lax.fori_loop(0, z.seqs, finish, stats)
    turned = jnp.transpose(jnp.concatenate([stats, jnp.zeros((LANES - z.queries, LANES), f32)], axis=0))
    lane_s = lax.broadcasted_iota(jnp.int32, (z.seqs, LANES), 1)
    both = jnp.where(lane_s < LANES // 2, turned[0 : z.seqs], pltpu.roll(turned[z.seqs : 2 * z.seqs], LANES // 2, 1))
    for b in range(z.seqs):
        stat[b] = both[b : b + 1]

    ld_vu.wait()

    def project(i, carry):
        xs = []
        for e in range(2):
            place = e * z.pairs + i
            xs.append(
                jnp.concatenate(
                    [ot[pl.ds(c * span + place, z.rows, stride=z.head_stride), :] for c in range(z.chunks)], axis=1
                )
            )
        x = jnp.concatenate(xs, axis=0).astype(bf16)
        w = jnp.concatenate([vu[2 * i], vu[2 * i + 1]], axis=1)
        y = jnp.dot(x, w, preferred_element_type=f32)
        for e in range(2):
            yt[pl.ds(e * z.pairs + i, z.rows, stride=z.head_stride), :] = y[
                e * z.rows : (e + 1) * z.rows, e * z.value : (e + 1) * z.value
            ]
        return carry

    lax.fori_loop(0, z.pairs, project, 0, unroll=2)

    def packed(r, carry):
        send[r] = yt[pl.ds(pl.multiple_of(r * z.head_stride, 8), z.heads), :].astype(bf16)
        return carry

    lax.fori_loop(0, z.rows, packed, 0, unroll=2)

    def sums_copy(i, q, row, source, sender_core):
        return pltpu.make_async_remote_copy(
            src_ref=send.at[row], dst_ref=recv.at[source], send_sem=es_sem.at[2 * i + q],
            recv_sem=er_sem.at[2 * i + sender_core], device_id={"ctx": row}, device_id_type=MESH,
        )

    def stat_copy(i, q, row, source, sender_core):
        return pltpu.make_async_remote_copy(
            src_ref=stat.at[row // CORES], dst_ref=statr.at[source], send_sem=ss_sem.at[2 * i + q],
            recv_sem=sr_sem.at[2 * i + sender_core], device_id={"ctx": row}, device_id_type=MESH,
        )

    others = [(i, q) for i in range(z.chips) for q in range(CORES) if (i, q) != (0, 0)]

    def target_row(i, q):
        return peer_chip(i) * CORES + (core if q == 0 else 1 - core)

    def source_row(i, q):
        return source_chip(i) * CORES + (core if q == 0 else 1 - core)

    for i, q in others:
        row = target_row(i, q)
        stat_copy(i, q, row, me, q).start()
        sums_copy(i, q, row, me, q).start()
    recv[me] = send[me]
    statr[me] = stat[chip]

    for i, q in others:
        stat_copy(i, q, me, source_row(i, q), q).wait_recv()
        sums_copy(i, q, me, source_row(i, q), q).wait_recv()

    s = jnp.concatenate([statr[d] for d in range(z.ctx)], axis=0)
    s = jnp.where(core == 0, s, pltpu.roll(s, LANES - z.heads, 1))
    t = pltpu.roll(s, LANES // 2, 1)
    top = jnp.max(s, axis=0, keepdims=True)
    factor = jnp.exp(s - top)
    total = jnp.sum(factor * t, axis=0, keepdims=True)
    lane_d = lax.broadcasted_iota(jnp.int32, (z.ctx, LANES), 1)
    share = jnp.where(lane_d < z.heads, factor / jnp.where(lane_d < z.heads, total, 1.0), 0.0)
    share = jnp.transpose(jnp.concatenate([share, jnp.zeros((LANES - z.ctx, LANES), f32)], axis=0))
    merged = jnp.zeros((z.heads, z.value), f32)
    for d in range(z.ctx):
        merged = merged + share[0 : z.heads, d : d + 1] * recv[d].astype(f32)
    acc[...] = merged
    for h in range(z.heads):
        at = (h % 2) * z.pairs + h // 2
        out_ref[:, h * z.value : (h + 1) * z.value] = acc[at : at + 1, :].astype(out_ref.dtype)

    for i in order:
        gather_copy(i, me).wait_send()
    for i in range(z.chips):
        forward_copy(i, source_chip(i) * CORES + core).wait_send()
    for i, q in others:
        row = target_row(i, q)
        stat_copy(i, q, row, me, q).wait_send()
        sums_copy(i, q, row, me, q).wait_send()


def per_device(
    query_nope, query_rope, cache_latent, cache_rope, key_up, value_up, lengths, block_owner, block_number,
):
    ctx = lax.axis_size("ctx")
    heads, nope, latent = key_up.shape
    slots, block, _ = cache_latent.shape
    z = Sizes(
        ctx, query_nope.shape[0] * ctx, heads, nope, query_rope.shape[1] // heads, latent, value_up.shape[2],
        slots, block, lengths.shape[0],
    )
    any_spec = pl.BlockSpec(memory_space=pl.ANY)
    V, S, D = pltpu.VMEM, pltpu.SMEM, pltpu.SemaphoreType.DMA
    span = z.rows * z.head_stride
    scratch = [
        V(query_nope.shape, bf16), V(query_rope.shape, bf16), V(cache_latent.shape, bf16), V(cache_rope.shape, bf16),
        V(key_up.shape, bf16), V(value_up.shape, bf16), S(lengths.shape, jnp.int32), S(block_owner.shape, jnp.int32),
        S(block_number.shape, jnp.int32), V((1, slots), jnp.int32), V((8, LANES), jnp.int32), S((8, LANES), jnp.int32),
        V((z.rows, z.block_rows, LANES), bf16),
        V((z.block_rows, LANES), f32),
        V((z.rows * z.gather_stride, LANES), f32),
        V((slots, z.key_stride, LANES), f32),
        V((z.chunks * span, LANES), f32),
        V((z.seqs, z.queries, latent), bf16),
        V((z.seqs, z.queries, LANES), f32),
        V((slots, z.queries, block), f32),
        V((slots, z.queries, block), f32),
        V((z.seqs, z.queries, block), f32),
        V((slots, z.queries, block), f32),
        V((slots, z.queries, latent), f32),
        V((z.chunks * span, LANES), f32),
        V((span, LANES), f32),
        V((z.rows, heads, z.value), bf16),
        V((z.ctx, heads, z.value), bf16),
        V((z.seqs, 1, LANES), f32),
        V((z.ctx, 1, LANES), f32),
        V((heads, z.value), f32),
        D((10,)), D, D((z.chips,)), D((z.chips,)), D((z.chips,)), D((z.chips,)),
        D((z.ctx,)), D((z.ctx,)), D((z.ctx,)), D((z.ctx,)),
    ]
    return pl.pallas_call(
        functools.partial(kernel, z),
        out_shape=jax.ShapeDtypeStruct((1, heads * z.value), bf16),
        in_specs=[any_spec] * 10,
        out_specs=pl.BlockSpec(memory_space=pltpu.VMEM),
        scratch_shapes=scratch,
        compiler_params=pltpu.CompilerParams(
            collective_id=0, has_side_effects=True, vmem_limit_bytes=64 * 1024 * 1024 - 65536
        ),
    )(
        query_nope, query_rope, cache_latent, cache_rope, key_up, value_up, lengths, block_owner,
        block_owner.reshape(1, slots), block_number,
    )


def solution(mesh):
    return jax.shard_map(
        per_device,
        mesh=mesh,
        in_specs=(
            P("ctx", "head"), P("ctx", "head"), P("ctx", None, None), P("ctx", None), P("head", None, None),
            P("head", None, None), P(), P("ctx"), P("ctx"),
        ),
        out_specs=P("ctx", "head"),
        check_vma=False,
    )
```

time: 211 us -> 42.8 us (0.20)
  matrix products: 73.6 us -> 0 us
  waiting for transfers between devices: 50.8 us -> 0 us
  Pallas kernels: 0 us -> 41.2 us
  local copies, waits for them, and re-layouts: 26.9 us -> 1.34 us
  other arithmetic: 25.5 us -> 0 us
  blocking collectives: 15.2 us -> 0 us
  between operations: 13.6 us -> 0.01 us
  starting transfers between devices: 5.34 us -> 0 us
    dot_general x8 -> x0, matrix products: 73.6 us -> none  [the longest x2 28.7 us: attend(): jnp.dot(weight.astype(jnp.bfloat16), key_latent, preferred_element_type=j...]
    all_gather x1 -> x0, waiting for transfers between devices: 43.3 us -> none  [sent_together(): lax.all_gather(both, axis, axis=dim, tiled=True)]
    pallas_call x0 -> x1, Pallas kernels: none -> 41.2 us  [per_device(): pl.pallas_call(functools.partial(kernel, z), out_shape=jax.ShapeDtypeStru...]
    reduce_sum x3 -> x0, other arithmetic: 22.5 us -> none  [the longest x2 22.4 us: attend(): part_total = jnp.sum(weight, axis=1)]
    reshape x10 -> x0, local copies, waits for them, and re-layouts: 18.5 us -> none  [the longest x2 15.5 us: attend(): jnp.broadcast_to(visible[:, None, :], (rows_all, head_part, key_count))]
    all_to_all x1 -> x0, blocking collectives: 15.2 us -> none  [summed_on_arrival(): lax.all_to_all(parts, axis, split_axis=0, concat_axis=0, tiled=True)]
    all_to_all x1 -> x0, waiting for transfers between devices: 7.53 us -> none  [copy_for_each(): return lax.all_to_all(copies, axis, split_axis=0, concat_axis=0, tiled=True)]
    all_to_all x1 -> x0, starting transfers between devices: 5.3 us -> none  [copy_for_each(): return lax.all_to_all(copies, axis, split_axis=0, concat_axis=0, tiled=True)]
  transfers between devices with their start and end apart: 2 -> 0, of which waited for: 2 -> 0; matrix products, arithmetic and copies ran while one was open for 2% -> 0% of each run, Pallas kernels for 0% -> 0%
where the time goes in v1:
time: 42.8 us; the launch traced here: 42.5 us
  Pallas kernels  41.2 us (96%)
  local copies, waits for them, and re-layouts  1.34 us (3%)
    pallas_call x1, Pallas kernels, per_device(): pl.pallas_call(functools.partial(kernel, z), out_shape=jax.ShapeDtypeStru...  41.2 us
    unnamed x1, local copies, waits for them, and re-layouts  1.34 us

profile of v1, /device:TPU:1, one launch (start us, length us, event | category | flops | bytes accessed | tf_op | source)
XLA Modules:
  0.0 42.5 jit_solution(9763798718841190004)
XLA Ops:
  0.0 41.2 %shard_map.91 = bf16[1,4096]{1,0:T(2,128)(2,1)} custom-call(bf16[1,4096]{1,0:T(2,128)(2,1)} %qn_hbm.1, bf16[1,2048]{1,0:T(2,128)(2,1)} %qr_hbm.1, bf16[64,128,512]{2,1,0:T(8,128)(2,1)} %lat_hbm.1, bf16[64,8192]{1,0:T(8,128)(2,1)} %kr_hbm.1, bf16[32,128,512]{2,1,0:T(8,128)(2,1)} %ku_hbm.1, bf16[32,512,128]{2,1,0:T(8,128)(2,1)} %vu_hbm.1, s32[16]{0:T(128)} %len_hbm.1, ...), custom_call_target="tpu_custom_call" | custom-call | tf_op jit(solution)/shard_map/pallas_call | solution.py:382
  41.2 1.3 %copy.11 = bf16[1,4096]{1,0:T(2,128)(2,1)} copy(bf16[1,4096]{1,0:T(2,128)(2,1)} %shard_map.91) | data formatting | bytes 16384

commit v2 on v1

--- a/solution.py
+++ b/solution.py
@@ -32,8 +32,8 @@
         self.queries = self.tokens * heads
         self.chunks = latent // LANES
         self.block_rows = heads + self.pairs
-        self.gather_stride = pad8(self.block_rows) + 8
-        self.head_stride = heads + 8
+        self.gather_stride = pad8(self.block_rows) + 4
+        self.head_stride = heads + 4
         self.key_stride = block + 8
 
 
@@ -51,11 +51,20 @@
     core = me - chip * CORES
     partner = chip * CORES + (1 - core)
 
+    side = math.isqrt(z.chips)
+    chip_x = chip // side
+    chip_z = chip - chip_x * side
+
     def peer_chip(i):
-        return lax.rem(chip + i, z.chips)
+        return lax.rem(chip_x + i // side, side) * side + lax.rem(chip_z + i % side, side)
 
     def source_chip(i):
-        return lax.rem(chip - i + z.chips, z.chips)
+        return lax.rem(chip_x + side - i // side, side) * side + lax.rem(chip_z + side - i % side, side)
+
+    def hops(i):
+        return min(i // side, side - i // side) + min(i % side, side - i % side)
+
+    far_first = sorted(range(z.chips), key=lambda i: -hops(i))
 
     loads = [
         pltpu.make_async_copy(s, d, load_sem.at[k])
@@ -98,7 +107,7 @@
             device_id={"ctx": partner}, device_id_type=MESH,
         )
 
-    order = list(range(1, z.chips))
+    order = [i for i in far_first if i]
     for i in order:
         gather_copy(i, me).start()
     forward_copy(0, me).start()
@@ -128,16 +137,16 @@
         rkf[pl.ds(2 * j + 1, n, stride=z.key_stride), :] = pltpu.roll(part, z.rope, 1)
         return carry
 
-    lax.fori_loop(0, z.block * z.rope // LANES, spread_keys, 0, unroll=2)
-
-    for i in order:
+    lax.fori_loop(0, z.block * z.rope // LANES, spread_keys, 0, unroll=4)
+
+    for i in order[::-1]:
         gather_copy(i, source_chip(i) * CORES + core).wait_recv()
         forward_copy(i, source_chip(i) * CORES + core).start()
     for i in range(z.chips):
         forward_copy(i, source_chip(i) * CORES + (1 - core)).wait_recv()
 
     def to_rows(r, carry):
-        gathf[pl.ds(pl.multiple_of(r * z.gather_stride, 8), z.block_rows), :] = gath[r].astype(f32)
+        gathf[pl.ds(r * z.gather_stride, z.block_rows), :] = gath[r].astype(f32)
         return carry
 
     lax.fori_loop(0, z.rows, to_rows, 0, unroll=2)
@@ -155,7 +164,7 @@
                 qlt[pl.ds(c * span + place, z.rows, stride=z.head_stride), :] = y[:, c * LANES : (c + 1) * LANES]
         return carry
 
-    lax.fori_loop(0, z.pairs, absorb, 0, unroll=2)
+    lax.fori_loop(0, z.pairs, absorb, 0, unroll=8)
 
     lane_p = lax.broadcasted_iota(jnp.int32, (z.pairs, LANES), 1)
 
@@ -163,17 +172,17 @@
         for j in range(z.tokens):
             r = b * z.tokens + j
             for c in range(z.chunks):
-                start = pl.multiple_of(c * span + r * z.head_stride, 8)
+                start = c * span + r * z.head_stride
                 ql[b, j * z.heads : (j + 1) * z.heads, c * LANES : (c + 1) * LANES] = qlt[
                     pl.ds(start, z.heads), :
                 ].astype(bf16)
-            both = gathf[pl.ds(pl.multiple_of(r * z.gather_stride + z.heads, 8), z.pairs), :]
+            both = gathf[pl.ds(r * z.gather_stride + z.heads, z.pairs), :]
             qro[b, j * z.heads : j * z.heads + z.pairs, :] = jnp.where(lane_p < z.rope, both, 0.0)
             other = pltpu.roll(both, z.rope, 1)
             qro[b, j * z.heads + z.pairs : (j + 1) * z.heads, :] = jnp.where(lane_p < z.rope, other, 0.0)
         return carry
 
-    lax.fori_loop(0, z.seqs, queries, 0)
+    lax.fori_loop(0, z.seqs, queries, 0, unroll=4)
 
     for c in (ld_len, ld_own, ld_num, ld_lat):
         c.wait()
@@ -182,23 +191,31 @@
     place = lax.broadcasted_iota(jnp.int32, (z.queries, z.block), 1) - token
     contract_last = (((1,), (1,)), ((), ()))
 
-    def score(j, carry):
+    def score(g, carry):
         top, before = carry
-        p = meta_s[0, j]
-        o = own_s[p]
-        b = jnp.maximum(o, 0)
-        limit = jnp.where(o >= 0, len_s[b] - (z.tokens - 1) - num_s[p] * z.block, -z.tokens)
-        s = lax.dot_general(ql[b], lat[p], contract_last, preferred_element_type=f32)
-        keys = rk[p, 0 : z.block, :]
-        s = s + lax.dot_general(qro[b], keys, contract_last, preferred_element_type=f32)
-        s = jnp.where(place < limit, s * score_scale, floor_value)
-        sc[j] = s
-        top = jnp.maximum(jnp.where(o == before, top, floor_value), s)
-        mpre[j] = top
-        return top, o
+        js = [2 * g, 2 * g + 1]
+        ps = [meta_s[0, j] for j in js]
+        os = [own_s[p] for p in ps]
+        bs = [jnp.maximum(o, 0) for o in os]
+        lhs = jnp.concatenate([ql[b] for b in bs], axis=0)
+        rhs = jnp.concatenate([lat[p] for p in ps], axis=0)
+        full = lax.dot_general(lhs, rhs, contract_last, preferred_element_type=f32)
+        lhs = jnp.concatenate([qro[b] for b in bs], axis=0)
+        rhs = jnp.concatenate([rk[p, 0 : z.block, :] for p in ps], axis=0)
+        full = full + lax.dot_general(lhs, rhs, contract_last, preferred_element_type=f32)
+        for u in range(2):
+            p, o, j = ps[u], os[u], js[u]
+            limit = jnp.where(o >= 0, len_s[bs[u]] - (z.tokens - 1) - num_s[p] * z.block, -z.tokens)
+            s = full[u * z.queries : (u + 1) * z.queries, u * z.block : (u + 1) * z.block]
+            s = jnp.where(place < limit, s * score_scale, floor_value)
+            sc[j] = s
+            top = jnp.maximum(jnp.where(o == before, top, floor_value), s)
+            mpre[j] = top
+            before = o
+        return top, before
 
     lax.fori_loop(
-        0, n, score, (jnp.full((z.queries, z.block), floor_value, f32), jnp.int32(-2)), unroll=4
+        0, n // 2, score, (jnp.full((z.queries, z.block), floor_value, f32), jnp.int32(-2)), unroll=8
     )
 
     lane_q = lax.broadcasted_iota(jnp.int32, (z.queries, LANES), 1)
@@ -218,10 +235,10 @@
         mtop[b] = jnp.broadcast_to(m, (z.queries, z.block))
         return jnp.where(lane_q == b, m, stats)
 
-    stats = lax.fori_loop(0, z.seqs, tops, jnp.zeros((z.queries, LANES), f32), unroll=2)
+    stats = lax.fori_loop(0, z.seqs, tops, jnp.zeros((z.queries, LANES), f32), unroll=4)
 
     def weigh(j, carry):
-        total, before = carry
+        total, run, before = carry
         p = meta_s[0, j]
         o = own_s[p]
         b = jnp.maximum(o, 0)
@@ -229,11 +246,11 @@
         keep = o == before
         total = jnp.where(keep, total, 0.0) + w
         lpre[j] = total
-        old = opre[jnp.maximum(j - 1, 0)]
-        opre[j] = jnp.where(keep, old, 0.0) + jnp.dot(w.astype(bf16), lat[p], preferred_element_type=f32)
-        return total, o
-
-    lax.fori_loop(0, n, weigh, (jnp.zeros((z.queries, z.block), f32), jnp.int32(-2)), unroll=4)
+        run = jnp.where(keep, run, 0.0) + jnp.dot(w.astype(bf16), lat[p], preferred_element_type=f32)
+        opre[j] = run
+        return total, run, o
+
+    lax.fori_loop(0, n, weigh, (jnp.zeros((z.queries, z.block), f32), jnp.zeros((z.queries, z.latent), f32), jnp.int32(-2)), unroll=16)
 
     def finish(b, stats):
         last, _ = segment(b)
@@ -241,13 +258,13 @@
         for j in range(z.tokens):
             r = b * z.tokens + j
             for c in range(z.chunks):
-                start = pl.multiple_of(c * span + r * z.head_stride, 8)
+                start = c * span + r * z.head_stride
                 ot[pl.ds(start, z.heads), :] = opre[
                     last, j * z.heads : (j + 1) * z.heads, c * LANES : (c + 1) * LANES
                 ]
         return jnp.where(lane_q == z.seqs + b, t, stats)
 
-    stats = lax.fori_loop(0, z.seqs, finish, stats)
+    stats = lax.fori_loop(0, z.seqs, finish, stats, unroll=4)
     turned = jnp.transpose(jnp.concatenate([stats, jnp.zeros((LANES - z.queries, LANES), f32)], axis=0))
     lane_s = lax.broadcasted_iota(jnp.int32, (z.seqs, LANES), 1)
     both = jnp.where(lane_s < LANES // 2, turned[0 : z.seqs], pltpu.roll(turned[z.seqs : 2 * z.seqs], LANES // 2, 1))
@@ -274,10 +291,10 @@
             ]
         return carry
 
-    lax.fori_loop(0, z.pairs, project, 0, unroll=2)
+    lax.fori_loop(0, z.pairs, project, 0, unroll=8)
 
     def packed(r, carry):
-        send[r] = yt[pl.ds(pl.multiple_of(r * z.head_stride, 8), z.heads), :].astype(bf16)
+        send[r] = yt[pl.ds(r * z.head_stride, z.heads), :].astype(bf16)
         return carry
 
     lax.fori_loop(0, z.rows, packed, 0, unroll=2)
@@ -294,7 +311,7 @@
             recv_sem=sr_sem.at[2 * i + sender_core], device_id={"ctx": row}, device_id_type=MESH,
         )
 
-    others = [(i, q) for i in range(z.chips) for q in range(CORES) if (i, q) != (0, 0)]
+    others = [(i, q) for i in far_first for q in range(CORES) if (i, q) != (0, 0)]
 
     def target_row(i, q):
         return peer_chip(i) * CORES + (core if q == 0 else 1 - core)

time: 42.8 us -> 34 us (0.79)
  Pallas kernels: 41.2 us -> 32.4 us
    pallas_call x1, Pallas kernels: 41.2 us -> 32.4 us  [per_device(): pl.pallas_call(functools.partial(kernel, z), out_shape=jax.ShapeDtypeStru...]
where the time goes in v2:
time: 34 us; the launch traced here: 33.8 us
  Pallas kernels  32.4 us (95%)
  local copies, waits for them, and re-layouts  1.34 us (4%)
    pallas_call x1, Pallas kernels, per_device(): pl.pallas_call(functools.partial(kernel, z), out_shape=jax.ShapeDtypeStru...  32.4 us
    unnamed x1, local copies, waits for them, and re-layouts  1.34 us

profile of v2, /device:TPU:1, one launch (start us, length us, event | category | flops | bytes accessed | tf_op | source)
XLA Modules:
  0.0 33.8 jit_solution(1613885950655048704)
XLA Ops:
  0.0 32.4 %shard_map.91 = bf16[1,4096]{1,0:T(2,128)(2,1)} custom-call(bf16[1,4096]{1,0:T(2,128)(2,1)} %qn_hbm.1, bf16[1,2048]{1,0:T(2,128)(2,1)} %qr_hbm.1, bf16[64,128,512]{2,1,0:T(8,128)(2,1)} %lat_hbm.1, bf16[64,8192]{1,0:T(8,128)(2,1)} %kr_hbm.1, bf16[32,128,512]{2,1,0:T(8,128)(2,1)} %ku_hbm.1, bf16[32,512,128]{2,1,0:T(8,128)(2,1)} %vu_hbm.1, s32[16]{0:T(128)} %len_hbm.1, ...), custom_call_target="tpu_custom_call" | custom-call | tf_op jit(solution)/shard_map/pallas_call | solution.py:399
  32.4 1.3 %copy.11 = bf16[1,4096]{1,0:T(2,128)(2,1)} copy(bf16[1,4096]{1,0:T(2,128)(2,1)} %shard_map.91) | data formatting | bytes 16384

commit v3 on v2

--- a/solution.py
+++ b/solution.py
@@ -42,9 +42,9 @@
     qn_hbm, qr_hbm, lat_hbm, kr_hbm, ku_hbm, vu_hbm, len_hbm, own_hbm, ownrow_hbm, num_hbm,
     out_ref,
     qn, qr, lat, kr, ku, vu, len_s, own_s, num_s, own_v, meta_v, meta_s,
-    gath, qstage, gathf, rk, qlt, ql, qro, sc, mpre, mtop, lpre, opre, ot, yt,
-    send, recv, stat, statr, acc,
-    load_sem, meta_sem, gs_sem, gr_sem, fs_sem, fr_sem, es_sem, er_sem, ss_sem, sr_sem,
+    gath, qstage, gathf, rk, kt, qlt, ql, qro, sc, mpre, mtop, mpart, lpre, opre, ot, yt,
+    sendp, part, send, recv, stat, statp, statf, statr, acc,
+    load_sem, meta_sem, ready, gs_sem, gr_sem, fs_sem, fr_sem, bs_sem, br_sem, fbs_sem, fbr_sem, ps_sem, pr_sem, es_sem, er_sem, ss_sem, sr_sem,
 ):
     me = lax.axis_index("ctx")
     chip = me // CORES
@@ -64,6 +64,21 @@
     def hops(i):
         return min(i // side, side - i // side) + min(i % side, side - i % side)
 
+    def layer(dz):
+        return lax.rem(chip_z + dz, side)
+
+    def source_layer(dz):
+        return lax.rem(chip_z + side - dz, side)
+
+    def on_layer(dz, test, act):
+        if dz:
+            pl.when(test(layer(dz)))(act)
+        else:
+            act()
+
+    def from_layer(dz, test, act):
+        pl.when(test(source_layer(dz)))(act)
+
     far_first = sorted(range(z.chips), key=lambda i: -hops(i))
 
     loads = [
@@ -79,11 +94,12 @@
 
     barrier = pltpu.get_barrier_semaphore()
     for i in range(z.chips):
-        for q in range(CORES):
-            target = peer_chip(i) * CORES + lax.rem(core + q, CORES)
-            if i == 0 and q == 0:
-                continue
+        target = peer_chip(i) * CORES + core if i else partner
+
+        def greet():
             pl.semaphore_signal(barrier, inc=1, device_id={"ctx": target}, device_id_type=MESH)
+
+        on_layer(i % side, lambda there: there > chip_z, greet)
 
     ld_qn.wait()
     ld_qr.wait()
@@ -91,26 +107,63 @@
         qstage[h : h + 1, :] = qn[:, h * LANES : (h + 1) * LANES].astype(f32)
     for h in range(z.pairs):
         qstage[z.heads + h : z.heads + h + 1, :] = qr[:, h * LANES : (h + 1) * LANES].astype(f32)
-    gath[me] = qstage[...].astype(bf16)
-
-    pl.semaphore_wait(barrier, z.ctx - 1)
-
-    def gather_copy(i, row):
-        return pltpu.make_async_remote_copy(
-            src_ref=gath.at[row], dst_ref=gath.at[row], send_sem=gs_sem.at[i], recv_sem=gr_sem.at[i],
+    own_slot = core * z.chips + chip_z * side + chip_x
+    gath[own_slot] = qstage[...].astype(bf16)
+
+    pl.semaphore_wait(barrier, side + side * chip_z)
+
+    def slot_of(i, which):
+        return which * z.chips + source_layer(i % side) * side + lax.rem(chip_x + side - i // side, side)
+
+    def gather_copy(i, slot):
+        return pltpu.make_async_remote_copy(
+            src_ref=gath.at[slot], dst_ref=gath.at[slot], send_sem=gs_sem.at[i], recv_sem=gr_sem.at[i],
             device_id={"ctx": peer_chip(i) * CORES + core}, device_id_type=MESH,
         )
 
-    def forward_copy(i, row):
-        return pltpu.make_async_remote_copy(
-            src_ref=gath.at[row], dst_ref=gath.at[row], send_sem=fs_sem.at[i], recv_sem=fr_sem.at[i],
+    def forward_copy(i, which):
+        return pltpu.make_async_remote_copy(
+            src_ref=gath.at[slot_of(i, which)], dst_ref=gath.at[slot_of(i, which)], send_sem=fs_sem.at[i],
+            recv_sem=fr_sem.at[i], device_id={"ctx": partner}, device_id_type=MESH,
+        )
+
+    def layer_rows(at, which):
+        return gath.at[pl.ds(which * z.chips + at * side, side)]
+
+    def layer_copy(dz, at):
+        return pltpu.make_async_remote_copy(
+            src_ref=layer_rows(at, core), dst_ref=layer_rows(at, core), send_sem=bs_sem.at[dz], recv_sem=br_sem.at[dz],
+            device_id={"ctx": (chip_x * side + layer(dz)) * CORES + core}, device_id_type=MESH,
+        )
+
+    def forward_layer(dz, which):
+        rows = layer_rows(source_layer(dz), which)
+        return pltpu.make_async_remote_copy(
+            src_ref=rows, dst_ref=rows, send_sem=fbs_sem.at[dz], recv_sem=fbr_sem.at[dz],
             device_id={"ctx": partner}, device_id_type=MESH,
         )
 
     order = [i for i in far_first if i]
+    level = [i for i in order if i % side == 0]
+    layers = range(1, side)
+
+    def lower(there):
+        return there < chip_z
+
+    def higher(there):
+        return there > chip_z
+
+    for dz in layers:
+
+        def tell():
+            pl.semaphore_signal(
+                ready.at[side - dz], inc=1, device_id={"ctx": (chip_x * side + layer(dz)) * CORES + core}, device_id_type=MESH
+            )
+
+        on_layer(dz, lower, tell)
     for i in order:
-        gather_copy(i, me).start()
-    forward_copy(0, me).start()
+        on_layer(i % side, lower, lambda: gather_copy(i, own_slot).start())
+    forward_copy(0, core).start()
 
     ld_ownv.wait()
     n = z.slots
@@ -139,17 +192,63 @@
 
     lax.fori_loop(0, z.block * z.rope // LANES, spread_keys, 0, unroll=4)
 
-    for i in order[::-1]:
-        gather_copy(i, source_chip(i) * CORES + core).wait_recv()
-        forward_copy(i, source_chip(i) * CORES + core).start()
-    for i in range(z.chips):
-        forward_copy(i, source_chip(i) * CORES + (1 - core)).wait_recv()
-
-    def to_rows(r, carry):
-        gathf[pl.ds(r * z.gather_stride, z.block_rows), :] = gath[r].astype(f32)
-        return carry
-
-    lax.fori_loop(0, z.rows, to_rows, 0, unroll=2)
+    def turn_keys(p, carry):
+        kt[p] = jnp.transpose(lat[p])
+        return carry
+
+    ld_lat.wait()
+    lax.fori_loop(0, n // 2, turn_keys, 0, unroll=2)
+
+    for i in level:
+        gather_copy(i, slot_of(i, core)).wait_recv()
+        forward_copy(i, core).start()
+    for dz in layers:
+
+        def hand_on():
+            pl.semaphore_wait(ready.at[dz], 1)
+            layer_copy(dz, chip_z).start()
+
+        on_layer(dz, higher, hand_on)
+
+    lax.fori_loop(n // 2, n - n // 4, turn_keys, 0, unroll=2)
+
+    for dz in layers:
+
+        def from_lower():
+            layer_copy(dz, source_layer(dz)).wait_recv()
+            forward_layer(dz, core).start()
+
+        def from_higher():
+            for i in order:
+                if i % side == dz:
+                    gather_copy(i, slot_of(i, core)).wait_recv()
+                    forward_copy(i, core).start()
+
+        from_layer(dz, lower, from_lower)
+        from_layer(dz, higher, from_higher)
+
+    lax.fori_loop(n - n // 4, n, turn_keys, 0, unroll=2)
+
+    forward_copy(0, 1 - core).wait_recv()
+    for i in level:
+        forward_copy(i, 1 - core).wait_recv()
+    for dz in layers:
+
+        def part_of_lower():
+            forward_layer(dz, 1 - core).wait_recv()
+
+        def part_of_higher():
+            for i in order:
+                if i % side == dz:
+                    forward_copy(i, 1 - core).wait_recv()
+
+        from_layer(dz, lower, part_of_lower)
+        from_layer(dz, higher, part_of_higher)
+
+    for chip_of in range(z.chips):
+        for which in range(CORES):
+            slot = which * z.chips + chip_of % side * side + chip_of // side
+            gathf[pl.ds((chip_of * CORES + which) * z.gather_stride, z.block_rows), :] = gath[slot].astype(f32)
 
     ld_ku.wait()
     span = z.rows * z.head_stride
@@ -184,7 +283,7 @@
 
     lax.fori_loop(0, z.seqs, queries, 0, unroll=4)
 
-    for c in (ld_len, ld_own, ld_num, ld_lat):
+    for c in (ld_len, ld_own, ld_num):
         c.wait()
     meta_copy.wait()
     token = lax.broadcasted_iota(jnp.int32, (z.queries, z.block), 0) // z.heads
@@ -198,8 +297,8 @@
         os = [own_s[p] for p in ps]
         bs = [jnp.maximum(o, 0) for o in os]
         lhs = jnp.concatenate([ql[b] for b in bs], axis=0)
-        rhs = jnp.concatenate([lat[p] for p in ps], axis=0)
-        full = lax.dot_general(lhs, rhs, contract_last, preferred_element_type=f32)
+        rhs = jnp.concatenate([kt[p] for p in ps], axis=1)
+        full = jnp.dot(lhs, rhs, preferred_element_type=f32)
         lhs = jnp.concatenate([qro[b] for b in bs], axis=0)
         rhs = jnp.concatenate([rk[p, 0 : z.block, :] for p in ps], axis=0)
         full = full + lax.dot_general(lhs, rhs, contract_last, preferred_element_type=f32)
@@ -228,14 +327,22 @@
         last, end = segment(b)
         return (end > 0) & (own_s[meta_s[0, last]] == b)
 
-    def tops(b, stats):
+    def tops(b, carry):
         last, _ = segment(b)
         m = jnp.max(mpre[last], axis=1, keepdims=True)
-        m = jnp.where(has_any(b), m, floor_value)
-        mtop[b] = jnp.broadcast_to(m, (z.queries, z.block))
-        return jnp.where(lane_q == b, m, stats)
-
-    stats = lax.fori_loop(0, z.seqs, tops, jnp.zeros((z.queries, LANES), f32), unroll=4)
+        mtop[b] = jnp.broadcast_to(jnp.where(has_any(b), m, floor_value), (z.queries, z.block))
+        return carry
+
+    lax.fori_loop(0, z.seqs, tops, 0, unroll=4)
+
+    def pair_copy(k, src, dst):
+        return pltpu.make_async_remote_copy(
+            src_ref=src, dst_ref=dst, send_sem=ps_sem.at[k], recv_sem=pr_sem.at[k],
+            device_id={"ctx": partner}, device_id_type=MESH,
+        )
+
+    top_copy = pair_copy(0, mtop, mpart)
+    top_copy.start()
 
     def weigh(j, carry):
         total, run, before = carry
@@ -252,26 +359,36 @@
 
     lax.fori_loop(0, n, weigh, (jnp.zeros((z.queries, z.block), f32), jnp.zeros((z.queries, z.latent), f32), jnp.int32(-2)), unroll=16)
 
+    top_copy.wait_recv()
+
     def finish(b, stats):
         last, _ = segment(b)
-        t = jnp.sum(lpre[last], axis=1, keepdims=True)
+        mine = mtop[b]
+        pair = jnp.maximum(mine, mpart[b])
+        scale = jnp.exp(mine - pair)
+        t = jnp.sum(lpre[last] * scale, axis=1, keepdims=True)
         for j in range(z.tokens):
             r = b * z.tokens + j
             for c in range(z.chunks):
                 start = c * span + r * z.head_stride
-                ot[pl.ds(start, z.heads), :] = opre[
-                    last, j * z.heads : (j + 1) * z.heads, c * LANES : (c + 1) * LANES
-                ]
+                ot[pl.ds(start, z.heads), :] = (
+                    opre[last, j * z.heads : (j + 1) * z.heads, c * LANES : (c + 1) * LANES]
+                    * scale[j * z.heads : (j + 1) * z.heads]
+                )
+        stats = jnp.where(lane_q == b, pair, stats)
         return jnp.where(lane_q == z.seqs + b, t, stats)
 
-    stats = lax.fori_loop(0, z.seqs, finish, stats, unroll=4)
+    stats = lax.fori_loop(0, z.seqs, finish, jnp.zeros((z.queries, LANES), f32), unroll=4)
     turned = jnp.transpose(jnp.concatenate([stats, jnp.zeros((LANES - z.queries, LANES), f32)], axis=0))
     lane_s = lax.broadcasted_iota(jnp.int32, (z.seqs, LANES), 1)
-    both = jnp.where(lane_s < LANES // 2, turned[0 : z.seqs], pltpu.roll(turned[z.seqs : 2 * z.seqs], LANES // 2, 1))
-    for b in range(z.seqs):
-        stat[b] = both[b : b + 1]
+    stat[...] = jnp.where(
+        lane_s < LANES // 2, turned[0 : z.seqs], pltpu.roll(turned[z.seqs : 2 * z.seqs], LANES // 2, 1)
+    )
+    stat_pair = pair_copy(1, stat, statp)
+    stat_pair.start()
 
     ld_vu.wait()
+    group = z.pairs // 2
 
     def project(i, carry):
         xs = []
@@ -291,56 +408,68 @@
             ]
         return carry
 
-    lax.fori_loop(0, z.pairs, project, 0, unroll=8)
-
-    def packed(r, carry):
-        send[r] = yt[pl.ds(r * z.head_stride, z.heads), :].astype(bf16)
-        return carry
-
-    lax.fori_loop(0, z.rows, packed, 0, unroll=2)
-
-    def sums_copy(i, q, row, source, sender_core):
-        return pltpu.make_async_remote_copy(
-            src_ref=send.at[row], dst_ref=recv.at[source], send_sem=es_sem.at[2 * i + q],
-            recv_sem=er_sem.at[2 * i + sender_core], device_id={"ctx": row}, device_id_type=MESH,
-        )
-
-    def stat_copy(i, q, row, source, sender_core):
-        return pltpu.make_async_remote_copy(
-            src_ref=stat.at[row // CORES], dst_ref=statr.at[source], send_sem=ss_sem.at[2 * i + q],
-            recv_sem=sr_sem.at[2 * i + sender_core], device_id={"ctx": row}, device_id_type=MESH,
-        )
-
-    others = [(i, q) for i in far_first for q in range(CORES) if (i, q) != (0, 0)]
-
-    def target_row(i, q):
-        return peer_chip(i) * CORES + (core if q == 0 else 1 - core)
-
-    def source_row(i, q):
-        return source_chip(i) * CORES + (core if q == 0 else 1 - core)
-
-    for i, q in others:
-        row = target_row(i, q)
-        stat_copy(i, q, row, me, q).start()
-        sums_copy(i, q, row, me, q).start()
-    recv[me] = send[me]
-    statr[me] = stat[chip]
-
-    for i, q in others:
-        stat_copy(i, q, me, source_row(i, q), q).wait_recv()
-        sums_copy(i, q, me, source_row(i, q), q).wait_recv()
-
-    s = jnp.concatenate([statr[d] for d in range(z.ctx)], axis=0)
+    sums_pair = []
+    for g in range(2):
+        lax.fori_loop(g * group, (g + 1) * group, project, 0, unroll=8)
+
+        def other_rows(k, carry):
+            base = (k * CORES + 1 - core) * z.head_stride + g * group
+            pieces = [yt[pl.ds(base + e * z.pairs, group), :] for e in range(2)]
+            sendp[g, k] = jnp.concatenate(pieces, axis=0).astype(bf16)
+            return carry
+
+        lax.fori_loop(0, z.chips, other_rows, 0, unroll=4)
+        sums_pair.append(pair_copy(2 + g, sendp.at[g], part.at[g]))
+        sums_pair[g].start()
+
+    stat_pair.wait_recv()
+    whole = jnp.where(lane_s < LANES // 2, stat[...], stat[...] + statp[...])
+    for b in range(z.seqs):
+        statf[b] = whole[b : b + 1]
+    for c in sums_pair:
+        c.wait_recv()
+
+    def own_rows(k, carry):
+        halves = [part[g, k].astype(f32) for g in range(2)]
+        theirs = jnp.concatenate([halves[g][e * group : (e + 1) * group] for e in range(2) for g in range(2)], axis=0)
+        send[k] = (yt[pl.ds((k * CORES + core) * z.head_stride, z.heads), :] + theirs).astype(bf16)
+        return carry
+
+    lax.fori_loop(0, z.chips, own_rows, 0, unroll=4)
+
+    def sums_copy(i, source):
+        return pltpu.make_async_remote_copy(
+            src_ref=send.at[peer_chip(i)], dst_ref=recv.at[source], send_sem=es_sem.at[i], recv_sem=er_sem.at[i],
+            device_id={"ctx": peer_chip(i) * CORES + core}, device_id_type=MESH,
+        )
+
+    def stat_copy(i, source):
+        return pltpu.make_async_remote_copy(
+            src_ref=statf.at[peer_chip(i)], dst_ref=statr.at[source], send_sem=ss_sem.at[i], recv_sem=sr_sem.at[i],
+            device_id={"ctx": peer_chip(i) * CORES + core}, device_id_type=MESH,
+        )
+
+    for i in order:
+        stat_copy(i, chip).start()
+        sums_copy(i, chip).start()
+    recv[chip] = send[chip]
+    statr[chip] = statf[chip]
+
+    for i in order:
+        stat_copy(i, source_chip(i)).wait_recv()
+        sums_copy(i, source_chip(i)).wait_recv()
+
+    s = jnp.concatenate([statr[d] for d in range(z.chips)], axis=0)
     s = jnp.where(core == 0, s, pltpu.roll(s, LANES - z.heads, 1))
     t = pltpu.roll(s, LANES // 2, 1)
     top = jnp.max(s, axis=0, keepdims=True)
     factor = jnp.exp(s - top)
     total = jnp.sum(factor * t, axis=0, keepdims=True)
-    lane_d = lax.broadcasted_iota(jnp.int32, (z.ctx, LANES), 1)
+    lane_d = lax.broadcasted_iota(jnp.int32, (z.chips, LANES), 1)
     share = jnp.where(lane_d < z.heads, factor / jnp.where(lane_d < z.heads, total, 1.0), 0.0)
-    share = jnp.transpose(jnp.concatenate([share, jnp.zeros((LANES - z.ctx, LANES), f32)], axis=0))
+    share = jnp.transpose(jnp.concatenate([share, jnp.zeros((LANES - z.chips, LANES), f32)], axis=0))
     merged = jnp.zeros((z.heads, z.value), f32)
-    for d in range(z.ctx):
+    for d in range(z.chips):
         merged = merged + share[0 : z.heads, d : d + 1] * recv[d].astype(f32)
     acc[...] = merged
     for h in range(z.heads):
@@ -348,13 +477,20 @@
         out_ref[:, h * z.value : (h + 1) * z.value] = acc[at : at + 1, :].astype(out_ref.dtype)
 
     for i in order:
-        gather_copy(i, me).wait_send()
-    for i in range(z.chips):
-        forward_copy(i, source_chip(i) * CORES + core).wait_send()
-    for i, q in others:
-        row = target_row(i, q)
-        stat_copy(i, q, row, me, q).wait_send()
-        sums_copy(i, q, row, me, q).wait_send()
+        on_layer(i % side, lower, lambda: gather_copy(i, own_slot).wait_send())
+    for i in [0] + level:
+        forward_copy(i, core).wait_send()
+    for dz in layers:
+        on_layer(dz, higher, lambda: layer_copy(dz, chip_z).wait_send())
+        from_layer(dz, lower, lambda: forward_layer(dz, core).wait_send())
+        for i in order:
+            if i % side == dz:
+                from_layer(dz, higher, lambda: forward_copy(i, core).wait_send())
+    for i in order:
+        stat_copy(i, chip).wait_send()
+        sums_copy(i, chip).wait_send()
+    for c in (top_copy, stat_pair, *sums_pair):
+        c.wait_send()
 
 
 def per_device(
@@ -370,6 +506,7 @@
     any_spec = pl.BlockSpec(memory_space=pl.ANY)
     V, S, D = pltpu.VMEM, pltpu.SMEM, pltpu.SemaphoreType.DMA
     span = z.rows * z.head_stride
+    side = math.isqrt(z.chips)
     scratch = [
         V(query_nope.shape, bf16), V(query_rope.shape, bf16), V(cache_latent.shape, bf16), V(cache_rope.shape, bf16),
         V(key_up.shape, bf16), V(value_up.shape, bf16), S(lengths.shape, jnp.int32), S(block_owner.shape, jnp.int32),
@@ -378,23 +515,31 @@
         V((z.block_rows, LANES), f32),
         V((z.rows * z.gather_stride, LANES), f32),
         V((slots, z.key_stride, LANES), f32),
+        V((slots, latent, block), bf16),
         V((z.chunks * span, LANES), f32),
         V((z.seqs, z.queries, latent), bf16),
         V((z.seqs, z.queries, LANES), f32),
         V((slots, z.queries, block), f32),
         V((slots, z.queries, block), f32),
         V((z.seqs, z.queries, block), f32),
+        V((z.seqs, z.queries, block), f32),
         V((slots, z.queries, block), f32),
         V((slots, z.queries, latent), f32),
         V((z.chunks * span, LANES), f32),
         V((span, LANES), f32),
-        V((z.rows, heads, z.value), bf16),
-        V((z.ctx, heads, z.value), bf16),
+        V((2, z.chips, heads // 2, z.value), bf16),
+        V((2, z.chips, heads // 2, z.value), bf16),
+        V((z.chips, heads, z.value), bf16),
+        V((z.chips, heads, z.value), bf16),
+        V((z.seqs, LANES), f32),
+        V((z.seqs, LANES), f32),
         V((z.seqs, 1, LANES), f32),
-        V((z.ctx, 1, LANES), f32),
+        V((z.chips, 1, LANES), f32),
         V((heads, z.value), f32),
-        D((10,)), D, D((z.chips,)), D((z.chips,)), D((z.chips,)), D((z.chips,)),
-        D((z.ctx,)), D((z.ctx,)), D((z.ctx,)), D((z.ctx,)),
+        D((10,)), D, pltpu.SemaphoreType.REGULAR((side,)), D((z.chips,)), D((z.chips,)), D((z.chips,)), D((z.chips,)),
+        D((side,)), D((side,)), D((side,)), D((side,)),
+        D((4,)), D((4,)),
+        D((z.chips,)), D((z.chips,)), D((z.chips,)), D((z.chips,)),
     ]
     return pl.pallas_call(
         functools.partial(kernel, z),

time: 34 us -> 32.9 us (0.968)
  Pallas kernels: 32.4 us -> 31.3 us
    pallas_call x1, Pallas kernels: 32.4 us -> 31.3 us  [per_device(): pl.pallas_call(functools.partial(kernel, z), out_shape=jax.ShapeDtypeStru...]
where the time goes in v3:
time: 32.9 us; the launch traced here: 32.7 us
  Pallas kernels  31.3 us (95%)
  local copies, waits for them, and re-layouts  1.34 us (4%)
    pallas_call x1, Pallas kernels, per_device(): pl.pallas_call(functools.partial(kernel, z), out_shape=jax.ShapeDtypeStru...  31.3 us
    unnamed x1, local copies, waits for them, and re-layouts  1.34 us

profile of v3, /device:TPU:1, one launch (start us, length us, event | category | flops | bytes accessed | tf_op | source)
XLA Modules:
  0.0 32.7 jit_solution(5293174026902079642)
XLA Ops:
  0.0 31.3 %shard_map.91 = bf16[1,4096]{1,0:T(2,128)(2,1)} custom-call(bf16[1,4096]{1,0:T(2,128)(2,1)} %qn_hbm.1, bf16[1,2048]{1,0:T(2,128)(2,1)} %qr_hbm.1, bf16[64,128,512]{2,1,0:T(8,128)(2,1)} %lat_hbm.1, bf16[64,8192]{1,0:T(8,128)(2,1)} %kr_hbm.1, bf16[32,128,512]{2,1,0:T(8,128)(2,1)} %ku_hbm.1, bf16[32,512,128]{2,1,0:T(8,128)(2,1)} %vu_hbm.1, s32[16]{0:T(128)} %len_hbm.1, ...), custom_call_target="tpu_custom_call" | custom-call | tf_op jit(solution)/shard_map/pallas_call | solution.py:544
  31.3 1.3 %copy.11 = bf16[1,4096]{1,0:T(2,128)(2,1)} copy(bf16[1,4096]{1,0:T(2,128)(2,1)} %shard_map.91) | data formatting | bytes 16384

commit v4 on v3

--- a/solution.py
+++ b/solution.py
@@ -43,8 +43,8 @@
     out_ref,
     qn, qr, lat, kr, ku, vu, len_s, own_s, num_s, own_v, meta_v, meta_s,
     gath, qstage, gathf, rk, kt, qlt, ql, qro, sc, mpre, mtop, mpart, lpre, opre, ot, yt,
-    sendp, part, send, recv, stat, statp, statf, statr, acc,
-    load_sem, meta_sem, ready, gs_sem, gr_sem, fs_sem, fr_sem, bs_sem, br_sem, fbs_sem, fbr_sem, ps_sem, pr_sem, es_sem, er_sem, ss_sem, sr_sem,
+    sendp, part, send, recv, stat, statp, statf, statr, acc, row_out,
+    out_sem, load_sem, meta_sem, gs_sem, gr_sem, fs_sem, fr_sem, ps_sem, pr_sem, es_sem, er_sem, ss_sem, sr_sem,
 ):
     me = lax.axis_index("ctx")
     chip = me // CORES
@@ -64,42 +64,27 @@
     def hops(i):
         return min(i // side, side - i // side) + min(i % side, side - i % side)
 
-    def layer(dz):
-        return lax.rem(chip_z + dz, side)
-
-    def source_layer(dz):
-        return lax.rem(chip_z + side - dz, side)
-
-    def on_layer(dz, test, act):
-        if dz:
-            pl.when(test(layer(dz)))(act)
-        else:
-            act()
-
-    def from_layer(dz, test, act):
-        pl.when(test(source_layer(dz)))(act)
-
     far_first = sorted(range(z.chips), key=lambda i: -hops(i))
 
+    piece = z.slots // 4
+    lat_parts = [
+        (lat_hbm.at[pl.ds(k * piece, piece)], lat.at[pl.ds(k * piece, piece)]) for k in range(4)
+    ]
     loads = [
         pltpu.make_async_copy(s, d, load_sem.at[k])
         for k, (s, d) in enumerate(
             [(qn_hbm, qn), (qr_hbm, qr), (ownrow_hbm, own_v), (len_hbm, len_s), (own_hbm, own_s),
-             (num_hbm, num_s), (kr_hbm, kr), (ku_hbm, ku), (lat_hbm, lat), (vu_hbm, vu)]
+             (num_hbm, num_s), (kr_hbm, kr), *lat_parts, (ku_hbm, ku), (vu_hbm, vu)]
         )
     ]
-    ld_qn, ld_qr, ld_ownv, ld_len, ld_own, ld_num, ld_kr, ld_ku, ld_lat, ld_vu = loads
+    ld_qn, ld_qr, ld_ownv, ld_len, ld_own, ld_num, ld_kr, *ld_lat, ld_ku, ld_vu = loads
     for c in loads:
         c.start()
 
     barrier = pltpu.get_barrier_semaphore()
     for i in range(z.chips):
         target = peer_chip(i) * CORES + core if i else partner
-
-        def greet():
-            pl.semaphore_signal(barrier, inc=1, device_id={"ctx": target}, device_id_type=MESH)
-
-        on_layer(i % side, lambda there: there > chip_z, greet)
+        pl.semaphore_signal(barrier, inc=1, device_id={"ctx": target}, device_id_type=MESH)
 
     ld_qn.wait()
     ld_qr.wait()
@@ -107,63 +92,35 @@
         qstage[h : h + 1, :] = qn[:, h * LANES : (h + 1) * LANES].astype(f32)
     for h in range(z.pairs):
         qstage[z.heads + h : z.heads + h + 1, :] = qr[:, h * LANES : (h + 1) * LANES].astype(f32)
-    own_slot = core * z.chips + chip_z * side + chip_x
-    gath[own_slot] = qstage[...].astype(bf16)
-
-    pl.semaphore_wait(barrier, side + side * chip_z)
-
-    def slot_of(i, which):
-        return which * z.chips + source_layer(i % side) * side + lax.rem(chip_x + side - i // side, side)
-
-    def gather_copy(i, slot):
+    gath[core * z.chips + chip] = qstage[...].astype(bf16)
+
+    pl.semaphore_wait(barrier, z.chips)
+
+    own_slot = core * z.chips + chip
+
+    def gather_copy(i):
         return pltpu.make_async_remote_copy(
-            src_ref=gath.at[slot], dst_ref=gath.at[slot], send_sem=gs_sem.at[i], recv_sem=gr_sem.at[i],
+            src_ref=gath.at[own_slot], dst_ref=gath.at[own_slot], send_sem=gs_sem, recv_sem=gr_sem,
             device_id={"ctx": peer_chip(i) * CORES + core}, device_id_type=MESH,
         )
 
-    def forward_copy(i, which):
+    def all_copies(src, dst, send_sem, recv_sem):
+        some = pl.ds(0, z.chips - 1)
         return pltpu.make_async_remote_copy(
-            src_ref=gath.at[slot_of(i, which)], dst_ref=gath.at[slot_of(i, which)], send_sem=fs_sem.at[i],
-            recv_sem=fr_sem.at[i], device_id={"ctx": partner}, device_id_type=MESH,
-        )
-
-    def layer_rows(at, which):
-        return gath.at[pl.ds(which * z.chips + at * side, side)]
-
-    def layer_copy(dz, at):
-        return pltpu.make_async_remote_copy(
-            src_ref=layer_rows(at, core), dst_ref=layer_rows(at, core), send_sem=bs_sem.at[dz], recv_sem=br_sem.at[dz],
-            device_id={"ctx": (chip_x * side + layer(dz)) * CORES + core}, device_id_type=MESH,
-        )
-
-    def forward_layer(dz, which):
-        rows = layer_rows(source_layer(dz), which)
-        return pltpu.make_async_remote_copy(
-            src_ref=rows, dst_ref=rows, send_sem=fbs_sem.at[dz], recv_sem=fbr_sem.at[dz],
+            src_ref=src.at[some], dst_ref=dst.at[some], send_sem=send_sem, recv_sem=recv_sem,
             device_id={"ctx": partner}, device_id_type=MESH,
         )
 
+    all_rows = all_copies(gath, gath, gs_sem, gr_sem)
+    half_rows = gath.at[pl.ds(core * z.chips, z.chips)]
+    forward = pltpu.make_async_remote_copy(
+        src_ref=half_rows, dst_ref=half_rows, send_sem=fs_sem, recv_sem=fr_sem,
+        device_id={"ctx": partner}, device_id_type=MESH,
+    )
+
     order = [i for i in far_first if i]
-    level = [i for i in order if i % side == 0]
-    layers = range(1, side)
-
-    def lower(there):
-        return there < chip_z
-
-    def higher(there):
-        return there > chip_z
-
-    for dz in layers:
-
-        def tell():
-            pl.semaphore_signal(
-                ready.at[side - dz], inc=1, device_id={"ctx": (chip_x * side + layer(dz)) * CORES + core}, device_id_type=MESH
-            )
-
-        on_layer(dz, lower, tell)
     for i in order:
-        on_layer(i % side, lower, lambda: gather_copy(i, own_slot).start())
-    forward_copy(0, core).start()
+        gather_copy(i).start()
 
     ld_ownv.wait()
     n = z.slots
@@ -196,59 +153,20 @@
         kt[p] = jnp.transpose(lat[p])
         return carry
 
-    ld_lat.wait()
-    lax.fori_loop(0, n // 2, turn_keys, 0, unroll=2)
-
-    for i in level:
-        gather_copy(i, slot_of(i, core)).wait_recv()
-        forward_copy(i, core).start()
-    for dz in layers:
-
-        def hand_on():
-            pl.semaphore_wait(ready.at[dz], 1)
-            layer_copy(dz, chip_z).start()
-
-        on_layer(dz, higher, hand_on)
-
-    lax.fori_loop(n // 2, n - n // 4, turn_keys, 0, unroll=2)
-
-    for dz in layers:
-
-        def from_lower():
-            layer_copy(dz, source_layer(dz)).wait_recv()
-            forward_layer(dz, core).start()
-
-        def from_higher():
-            for i in order:
-                if i % side == dz:
-                    gather_copy(i, slot_of(i, core)).wait_recv()
-                    forward_copy(i, core).start()
-
-        from_layer(dz, lower, from_lower)
-        from_layer(dz, higher, from_higher)
-
-    lax.fori_loop(n - n // 4, n, turn_keys, 0, unroll=2)
-
-    forward_copy(0, 1 - core).wait_recv()
-    for i in level:
-        forward_copy(i, 1 - core).wait_recv()
-    for dz in layers:
-
-        def part_of_lower():
-            forward_layer(dz, 1 - core).wait_recv()
-
-        def part_of_higher():
-            for i in order:
-                if i % side == dz:
-                    forward_copy(i, 1 - core).wait_recv()
-
-        from_layer(dz, lower, part_of_lower)
-        from_layer(dz, higher, part_of_higher)
-
-    for chip_of in range(z.chips):
-        for which in range(CORES):
-            slot = which * z.chips + chip_of % side * side + chip_of // side
-            gathf[pl.ds((chip_of * CORES + which) * z.gather_stride, z.block_rows), :] = gath[slot].astype(f32)
+    for k in range(3):
+        ld_lat[k].wait()
+        lax.fori_loop(k * piece, (k + 1) * piece, turn_keys, 0, unroll=2)
+
+    all_rows.wait_recv()
+    forward.start()
+
+    ld_lat[3].wait()
+    lax.fori_loop(3 * piece, 4 * piece, turn_keys, 0, unroll=2)
+
+    forward.wait_recv()
+
+    for row in range(z.rows):
+        gathf[pl.ds(row * z.gather_stride, z.block_rows), :] = gath[row % CORES * z.chips + row // CORES].astype(f32)
 
     ld_ku.wait()
     span = z.rows * z.head_stride
@@ -439,13 +357,13 @@
 
     def sums_copy(i, source):
         return pltpu.make_async_remote_copy(
-            src_ref=send.at[peer_chip(i)], dst_ref=recv.at[source], send_sem=es_sem.at[i], recv_sem=er_sem.at[i],
+            src_ref=send.at[peer_chip(i)], dst_ref=recv.at[source], send_sem=es_sem, recv_sem=er_sem,
             device_id={"ctx": peer_chip(i) * CORES + core}, device_id_type=MESH,
         )
 
     def stat_copy(i, source):
         return pltpu.make_async_remote_copy(
-            src_ref=statf.at[peer_chip(i)], dst_ref=statr.at[source], send_sem=ss_sem.at[i], recv_sem=sr_sem.at[i],
+            src_ref=statf.at[peer_chip(i)], dst_ref=statr.at[source], send_sem=ss_sem, recv_sem=sr_sem,
             device_id={"ctx": peer_chip(i) * CORES + core}, device_id_type=MESH,
         )
 
@@ -455,9 +373,10 @@
     recv[chip] = send[chip]
     statr[chip] = statf[chip]
 
-    for i in order:
-        stat_copy(i, source_chip(i)).wait_recv()
-        sums_copy(i, source_chip(i)).wait_recv()
+    all_stats = all_copies(statf, statr, ss_sem, sr_sem)
+    all_sums = all_copies(send, recv, es_sem, er_sem)
+    all_stats.wait_recv()
+    all_sums.wait_recv()
 
     s = jnp.concatenate([statr[d] for d in range(z.chips)], axis=0)
     s = jnp.where(core == 0, s, pltpu.roll(s, LANES - z.heads, 1))
@@ -474,23 +393,17 @@
     acc[...] = merged
     for h in range(z.heads):
         at = (h % 2) * z.pairs + h // 2
-        out_ref[:, h * z.value : (h + 1) * z.value] = acc[at : at + 1, :].astype(out_ref.dtype)
-
-    for i in order:
-        on_layer(i % side, lower, lambda: gather_copy(i, own_slot).wait_send())
-    for i in [0] + level:
-        forward_copy(i, core).wait_send()
-    for dz in layers:
-        on_layer(dz, higher, lambda: layer_copy(dz, chip_z).wait_send())
-        from_layer(dz, lower, lambda: forward_layer(dz, core).wait_send())
-        for i in order:
-            if i % side == dz:
-                from_layer(dz, higher, lambda: forward_copy(i, core).wait_send())
-    for i in order:
-        stat_copy(i, chip).wait_send()
-        sums_copy(i, chip).wait_send()
+        row_out[:, h * z.value : (h + 1) * z.value] = acc[at : at + 1, :].astype(out_ref.dtype)
+    out_copy = pltpu.make_async_copy(row_out, out_ref, out_sem)
+    out_copy.start()
+
+    all_rows.wait_send()
+    forward.wait_send()
+    all_stats.wait_send()
+    all_sums.wait_send()
     for c in (top_copy, stat_pair, *sums_pair):
         c.wait_send()
+    out_copy.wait()
 
 
 def per_device(
@@ -506,7 +419,6 @@
     any_spec = pl.BlockSpec(memory_space=pl.ANY)
     V, S, D = pltpu.VMEM, pltpu.SMEM, pltpu.SemaphoreType.DMA
     span = z.rows * z.head_stride
-    side = math.isqrt(z.chips)
     scratch = [
         V(query_nope.shape, bf16), V(query_rope.shape, bf16), V(cache_latent.shape, bf16), V(cache_rope.shape, bf16),
         V(key_up.shape, bf16), V(value_up.shape, bf16), S(lengths.shape, jnp.int32), S(block_owner.shape, jnp.int32),
@@ -536,16 +448,17 @@
         V((z.seqs, 1, LANES), f32),
         V((z.chips, 1, LANES), f32),
         V((heads, z.value), f32),
-        D((10,)), D, pltpu.SemaphoreType.REGULAR((side,)), D((z.chips,)), D((z.chips,)), D((z.chips,)), D((z.chips,)),
-        D((side,)), D((side,)), D((side,)), D((side,)),
+        V((1, heads * z.value), bf16),
+        D,
+        D((13,)), D, D, D, D, D,
         D((4,)), D((4,)),
-        D((z.chips,)), D((z.chips,)), D((z.chips,)), D((z.chips,)),
+        D, D, D, D,
     ]
     return pl.pallas_call(
         functools.partial(kernel, z),
         out_shape=jax.ShapeDtypeStruct((1, heads * z.value), bf16),
         in_specs=[any_spec] * 10,
-        out_specs=pl.BlockSpec(memory_space=pltpu.VMEM),
+        out_specs=any_spec,
         scratch_shapes=scratch,
         compiler_params=pltpu.CompilerParams(
             collective_id=0, has_side_effects=True, vmem_limit_bytes=64 * 1024 * 1024 - 65536

time: 32.9 us -> 30 us (0.912)
  Pallas kernels: 31.3 us -> 28.4 us
    pallas_call x1, Pallas kernels: 31.3 us -> 28.4 us  [per_device(): pl.pallas_call(functools.partial(kernel, z), out_shape=jax.ShapeDtypeStru...]
where the time goes in v4:
time: 30 us; the launch traced here: 29.8 us
  Pallas kernels  28.4 us (95%)
  local copies, waits for them, and re-layouts  1.34 us (4%)
    pallas_call x1, Pallas kernels, per_device(): pl.pallas_call(functools.partial(kernel, z), out_shape=jax.ShapeDtypeStru...  28.4 us
    unnamed x1, local copies, waits for them, and re-layouts  1.34 us

profile of v4, /device:TPU:1, one launch (start us, length us, event | category | flops | bytes accessed | tf_op | source)
XLA Modules:
  0.0 29.8 jit_solution(7032515985325504463)
XLA Ops:
  0.0 28.4 %shard_map.91 = bf16[1,4096]{1,0:T(2,128)(2,1)} custom-call(bf16[1,4096]{1,0:T(2,128)(2,1)} %qn_hbm.1, bf16[1,2048]{1,0:T(2,128)(2,1)} %qr_hbm.1, bf16[64,128,512]{2,1,0:T(8,128)(2,1)} %lat_hbm.1, bf16[64,8192]{1,0:T(8,128)(2,1)} %kr_hbm.1, bf16[32,128,512]{2,1,0:T(8,128)(2,1)} %ku_hbm.1, bf16[32,512,128]{2,1,0:T(8,128)(2,1)} %vu_hbm.1, s32[16]{0:T(128)} %len_hbm.1, ...), custom_call_target="tpu_custom_call" | custom-call | tf_op jit(solution)/shard_map/pallas_call | solution.py:457
  28.4 1.3 %copy.11 = bf16[1,4096]{1,0:T(2,128)(2,1)} copy(bf16[1,4096]{1,0:T(2,128)(2,1)} %shard_map.91) | data formatting | bytes 16384

commit v5 on v4

--- a/solution.py
+++ b/solution.py
@@ -43,7 +43,7 @@
     out_ref,
     qn, qr, lat, kr, ku, vu, len_s, own_s, num_s, own_v, meta_v, meta_s,
     gath, qstage, gathf, rk, kt, qlt, ql, qro, sc, mpre, mtop, mpart, lpre, opre, ot, yt,
-    sendp, part, send, recv, stat, statp, statf, statr, acc, row_out,
+    sendp, part, send, recv, stat, statp, statf, statr, shares, acc, row_out,
     out_sem, load_sem, meta_sem, gs_sem, gr_sem, fs_sem, fr_sem, ps_sem, pr_sem, es_sem, er_sem, ss_sem, sr_sem,
 ):
     me = lax.axis_index("ctx")
@@ -119,8 +119,16 @@
     )
 
     order = [i for i in far_first if i]
-    for i in order:
-        gather_copy(i).start()
+    late_first = sorted(range(z.chips), key=lambda k: (-(k % side), k // side in (0, 1)))
+    for k in late_first:
+
+        def give():
+            pltpu.make_async_remote_copy(
+                src_ref=gath.at[own_slot], dst_ref=gath.at[own_slot], send_sem=gs_sem, recv_sem=gr_sem,
+                device_id={"ctx": k * CORES + core}, device_id_type=MESH,
+            ).start()
+
+        pl.when(chip != k)(give)
 
     ld_ownv.wait()
     n = z.slots
@@ -199,7 +207,7 @@
             qro[b, j * z.heads + z.pairs : (j + 1) * z.heads, :] = jnp.where(lane_p < z.rope, other, 0.0)
         return carry
 
-    lax.fori_loop(0, z.seqs, queries, 0, unroll=4)
+    lax.fori_loop(0, z.seqs, queries, 0, unroll=16)
 
     for c in (ld_len, ld_own, ld_num):
         c.wait()
@@ -251,7 +259,7 @@
         mtop[b] = jnp.broadcast_to(jnp.where(has_any(b), m, floor_value), (z.queries, z.block))
         return carry
 
-    lax.fori_loop(0, z.seqs, tops, 0, unroll=4)
+    lax.fori_loop(0, z.seqs, tops, 0, unroll=16)
 
     def pair_copy(k, src, dst):
         return pltpu.make_async_remote_copy(
@@ -296,7 +304,7 @@
         stats = jnp.where(lane_q == b, pair, stats)
         return jnp.where(lane_q == z.seqs + b, t, stats)
 
-    stats = lax.fori_loop(0, z.seqs, finish, jnp.zeros((z.queries, LANES), f32), unroll=4)
+    stats = lax.fori_loop(0, z.seqs, finish, jnp.zeros((z.queries, LANES), f32), unroll=8)
     turned = jnp.transpose(jnp.concatenate([stats, jnp.zeros((LANES - z.queries, LANES), f32)], axis=0))
     lane_s = lax.broadcasted_iota(jnp.int32, (z.seqs, LANES), 1)
     stat[...] = jnp.where(
@@ -340,10 +348,25 @@
         sums_pair.append(pair_copy(2 + g, sendp.at[g], part.at[g]))
         sums_pair[g].start()
 
+    def sums_copy(i, source):
+        return pltpu.make_async_remote_copy(
+            src_ref=send.at[peer_chip(i)], dst_ref=recv.at[source], send_sem=es_sem, recv_sem=er_sem,
+            device_id={"ctx": peer_chip(i) * CORES + core}, device_id_type=MESH,
+        )
+
+    def stat_copy(i, source):
+        return pltpu.make_async_remote_copy(
+            src_ref=statf.at[peer_chip(i)], dst_ref=statr.at[source], send_sem=ss_sem, recv_sem=sr_sem,
+            device_id={"ctx": peer_chip(i) * CORES + core}, device_id_type=MESH,
+        )
+
     stat_pair.wait_recv()
     whole = jnp.where(lane_s < LANES // 2, stat[...], stat[...] + statp[...])
     for b in range(z.seqs):
         statf[b] = whole[b : b + 1]
+    for i in order:
+        stat_copy(i, chip).start()
+    statr[chip] = statf[chip]
     for c in sums_pair:
         c.wait_recv()
 
@@ -355,28 +378,13 @@
 
     lax.fori_loop(0, z.chips, own_rows, 0, unroll=4)
 
-    def sums_copy(i, source):
-        return pltpu.make_async_remote_copy(
-            src_ref=send.at[peer_chip(i)], dst_ref=recv.at[source], send_sem=es_sem, recv_sem=er_sem,
-            device_id={"ctx": peer_chip(i) * CORES + core}, device_id_type=MESH,
-        )
-
-    def stat_copy(i, source):
-        return pltpu.make_async_remote_copy(
-            src_ref=statf.at[peer_chip(i)], dst_ref=statr.at[source], send_sem=ss_sem, recv_sem=sr_sem,
-            device_id={"ctx": peer_chip(i) * CORES + core}, device_id_type=MESH,
-        )
-
     for i in order:
-        stat_copy(i, chip).start()
         sums_copy(i, chip).start()
     recv[chip] = send[chip]
-    statr[chip] = statf[chip]
 
     all_stats = all_copies(statf, statr, ss_sem, sr_sem)
     all_sums = all_copies(send, recv, es_sem, er_sem)
     all_stats.wait_recv()
-    all_sums.wait_recv()
 
     s = jnp.concatenate([statr[d] for d in range(z.chips)], axis=0)
     s = jnp.where(core == 0, s, pltpu.roll(s, LANES - z.heads, 1))
@@ -387,9 +395,11 @@
     lane_d = lax.broadcasted_iota(jnp.int32, (z.chips, LANES), 1)
     share = jnp.where(lane_d < z.heads, factor / jnp.where(lane_d < z.heads, total, 1.0), 0.0)
     share = jnp.transpose(jnp.concatenate([share, jnp.zeros((LANES - z.chips, LANES), f32)], axis=0))
+    shares[...] = share
+    all_sums.wait_recv()
     merged = jnp.zeros((z.heads, z.value), f32)
     for d in range(z.chips):
-        merged = merged + share[0 : z.heads, d : d + 1] * recv[d].astype(f32)
+        merged = merged + shares[0 : z.heads, d : d + 1] * recv[d].astype(f32)
     acc[...] = merged
     for h in range(z.heads):
         at = (h % 2) * z.pairs + h // 2
@@ -447,6 +457,7 @@
         V((z.seqs, LANES), f32),
         V((z.seqs, 1, LANES), f32),
         V((z.chips, 1, LANES), f32),
+        V((LANES, LANES), f32),
         V((heads, z.value), f32),
         V((1, heads * z.value), bf16),
         D,

time: 30 us -> 28.6 us (0.953)
  Pallas kernels: 28.4 us -> 27 us
    pallas_call x1, Pallas kernels: 28.4 us -> 27 us  [per_device(): pl.pallas_call(functools.partial(kernel, z), out_shape=jax.ShapeDtypeStru...]
where the time goes in v5:
time: 28.6 us; the launch traced here: 28.3 us
  Pallas kernels  27 us (94%)
  local copies, waits for them, and re-layouts  1.34 us (5%)
    pallas_call x1, Pallas kernels, per_device(): pl.pallas_call(functools.partial(kernel, z), out_shape=jax.ShapeDtypeStru...  27 us
    unnamed x1, local copies, waits for them, and re-layouts  1.34 us

profile of v5, /device:TPU:1, one launch (start us, length us, event | category | flops | bytes accessed | tf_op | source)
XLA Modules:
  0.0 28.3 jit_solution(1768963411008644784)
XLA Ops:
  0.0 27.0 %shard_map.91 = bf16[1,4096]{1,0:T(2,128)(2,1)} custom-call(bf16[1,4096]{1,0:T(2,128)(2,1)} %qn_hbm.1, bf16[1,2048]{1,0:T(2,128)(2,1)} %qr_hbm.1, bf16[64,128,512]{2,1,0:T(8,128)(2,1)} %lat_hbm.1, bf16[64,8192]{1,0:T(8,128)(2,1)} %kr_hbm.1, bf16[32,128,512]{2,1,0:T(8,128)(2,1)} %ku_hbm.1, bf16[32,512,128]{2,1,0:T(8,128)(2,1)} %vu_hbm.1, s32[16]{0:T(128)} %len_hbm.1, ...), custom_call_target="tpu_custom_call" | custom-call | tf_op jit(solution)/shard_map/pallas_call | solution.py:468
  27.0 1.3 %copy.11 = bf16[1,4096]{1,0:T(2,128)(2,1)} copy(bf16[1,4096]{1,0:T(2,128)(2,1)} %shard_map.91) | data formatting | bytes 16384

commit v6 on v5

--- a/solution.py
+++ b/solution.py
@@ -42,7 +42,7 @@
     qn_hbm, qr_hbm, lat_hbm, kr_hbm, ku_hbm, vu_hbm, len_hbm, own_hbm, ownrow_hbm, num_hbm,
     out_ref,
     qn, qr, lat, kr, ku, vu, len_s, own_s, num_s, own_v, meta_v, meta_s,
-    gath, qstage, gathf, rk, kt, qlt, ql, qro, sc, mpre, mtop, mpart, lpre, opre, ot, yt,
+    gath, qstage, gathf, rk, kt, qlt, ql, qro, sc, mpre, mtop, mtwo, mpart, lpre, opre, ot, yt,
     sendp, part, send, recv, stat, statp, statf, statr, shares, acc, row_out,
     out_sem, load_sem, meta_sem, gs_sem, gr_sem, fs_sem, fr_sem, ps_sem, pr_sem, es_sem, er_sem, ss_sem, sr_sem,
 ):
@@ -119,16 +119,23 @@
     )
 
     order = [i for i in far_first if i]
-    late_first = sorted(range(z.chips), key=lambda k: (-(k % side), k // side in (0, 1)))
-    for k in late_first:
-
-        def give():
-            pltpu.make_async_remote_copy(
-                src_ref=gath.at[own_slot], dst_ref=gath.at[own_slot], send_sem=gs_sem, recv_sem=gr_sem,
-                device_id={"ctx": k * CORES + core}, device_id_type=MESH,
-            ).start()
-
-        pl.when(chip != k)(give)
+    def give(target):
+        pltpu.make_async_remote_copy(
+            src_ref=gath.at[own_slot], dst_ref=gath.at[own_slot], send_sem=gs_sem, recv_sem=gr_sem,
+            device_id={"ctx": target * CORES + core}, device_id_type=MESH,
+        ).start()
+
+    def early():
+        for k in sorted(range(z.chips), key=lambda k: (-(k % side), k // side in (0, 1))):
+            pl.when(chip != k)(functools.partial(give, k))
+
+    def late():
+        for i in order:
+            give(peer_chip(i))
+
+    is_late = chip_z >= side // 2
+    pl.when(is_late)(late)
+    pl.when(jnp.logical_not(is_late))(early)
 
     ld_ownv.wait()
     n = z.slots
@@ -189,7 +196,7 @@
                 qlt[pl.ds(c * span + place, z.rows, stride=z.head_stride), :] = y[:, c * LANES : (c + 1) * LANES]
         return carry
 
-    lax.fori_loop(0, z.pairs, absorb, 0, unroll=8)
+    lax.fori_loop(0, z.pairs, absorb, 0, unroll=16)
 
     lane_p = lax.broadcasted_iota(jnp.int32, (z.pairs, LANES), 1)
 
@@ -202,9 +209,9 @@
                     pl.ds(start, z.heads), :
                 ].astype(bf16)
             both = gathf[pl.ds(r * z.gather_stride + z.heads, z.pairs), :]
-            qro[b, j * z.heads : j * z.heads + z.pairs, :] = jnp.where(lane_p < z.rope, both, 0.0)
+            qro[b, j * z.heads : j * z.heads + z.pairs, :] = jnp.where(lane_p < z.rope, both, 0.0).astype(bf16)
             other = pltpu.roll(both, z.rope, 1)
-            qro[b, j * z.heads + z.pairs : (j + 1) * z.heads, :] = jnp.where(lane_p < z.rope, other, 0.0)
+            qro[b, j * z.heads + z.pairs : (j + 1) * z.heads, :] = jnp.where(lane_p < z.rope, other, 0.0).astype(bf16)
         return carry
 
     lax.fori_loop(0, z.seqs, queries, 0, unroll=16)
@@ -226,7 +233,7 @@
         rhs = jnp.concatenate([kt[p] for p in ps], axis=1)
         full = jnp.dot(lhs, rhs, preferred_element_type=f32)
         lhs = jnp.concatenate([qro[b] for b in bs], axis=0)
-        rhs = jnp.concatenate([rk[p, 0 : z.block, :] for p in ps], axis=0)
+        rhs = jnp.concatenate([rk[p, 0 : z.block, :] for p in ps], axis=0).astype(bf16)
         full = full + lax.dot_general(lhs, rhs, contract_last, preferred_element_type=f32)
         for u in range(2):
             p, o, j = ps[u], os[u], js[u]
@@ -240,7 +247,7 @@
         return top, before
 
     lax.fori_loop(
-        0, n // 2, score, (jnp.full((z.queries, z.block), floor_value, f32), jnp.int32(-2)), unroll=8
+        0, n // 2, score, (jnp.full((z.queries, z.block), floor_value, f32), jnp.int32(-2)), unroll=32
     )
 
     lane_q = lax.broadcasted_iota(jnp.int32, (z.queries, LANES), 1)
@@ -253,13 +260,20 @@
         last, end = segment(b)
         return (end > 0) & (own_s[meta_s[0, last]] == b)
 
-    def tops(b, carry):
-        last, _ = segment(b)
-        m = jnp.max(mpre[last], axis=1, keepdims=True)
-        mtop[b] = jnp.broadcast_to(jnp.where(has_any(b), m, floor_value), (z.queries, z.block))
-        return carry
-
-    lax.fori_loop(0, z.seqs, tops, 0, unroll=16)
+    low_q = lane_q < LANES // 2
+
+    def tops(g, carry):
+        two = []
+        for b in (2 * g, 2 * g + 1):
+            last, _ = segment(b)
+            m = jnp.max(mpre[last], axis=1, keepdims=True)
+            m = jnp.broadcast_to(jnp.where(has_any(b), m, floor_value), (z.queries, z.block))
+            mtop[b] = m
+            two.append(m)
+        mtwo[g] = jnp.where(low_q, two[0], two[1])
+        return carry
+
+    lax.fori_loop(0, z.seqs // 2, tops, 0, unroll=8)
 
     def pair_copy(k, src, dst):
         return pltpu.make_async_remote_copy(
@@ -267,7 +281,7 @@
             device_id={"ctx": partner}, device_id_type=MESH,
         )
 
-    top_copy = pair_copy(0, mtop, mpart)
+    top_copy = pair_copy(0, mtwo, mpart)
     top_copy.start()
 
     def weigh(j, carry):
@@ -283,28 +297,33 @@
         opre[j] = run
         return total, run, o
 
-    lax.fori_loop(0, n, weigh, (jnp.zeros((z.queries, z.block), f32), jnp.zeros((z.queries, z.latent), f32), jnp.int32(-2)), unroll=16)
+    lax.fori_loop(0, n, weigh, (jnp.zeros((z.queries, z.block), f32), jnp.zeros((z.queries, z.latent), f32), jnp.int32(-2)), unroll=64)
 
     top_copy.wait_recv()
 
-    def finish(b, stats):
-        last, _ = segment(b)
-        mine = mtop[b]
-        pair = jnp.maximum(mine, mpart[b])
-        scale = jnp.exp(mine - pair)
-        t = jnp.sum(lpre[last] * scale, axis=1, keepdims=True)
-        for j in range(z.tokens):
-            r = b * z.tokens + j
-            for c in range(z.chunks):
-                start = c * span + r * z.head_stride
-                ot[pl.ds(start, z.heads), :] = (
-                    opre[last, j * z.heads : (j + 1) * z.heads, c * LANES : (c + 1) * LANES]
-                    * scale[j * z.heads : (j + 1) * z.heads]
-                )
-        stats = jnp.where(lane_q == b, pair, stats)
-        return jnp.where(lane_q == z.seqs + b, t, stats)
-
-    stats = lax.fori_loop(0, z.seqs, finish, jnp.zeros((z.queries, LANES), f32), unroll=8)
+    def finish(g, stats):
+        two = mpart[g]
+        swapped = pltpu.roll(two, LANES // 2, 1)
+        for e in range(2):
+            b = 2 * g + e
+            last, _ = segment(b)
+            mine = mtop[b]
+            pair = jnp.maximum(mine, jnp.where(low_q, two, swapped) if e == 0 else jnp.where(low_q, swapped, two))
+            scale = jnp.exp(mine - pair)
+            t = jnp.sum(lpre[last] * scale, axis=1, keepdims=True)
+            for j in range(z.tokens):
+                r = b * z.tokens + j
+                for c in range(z.chunks):
+                    start = c * span + r * z.head_stride
+                    ot[pl.ds(start, z.heads), :] = (
+                        opre[last, j * z.heads : (j + 1) * z.heads, c * LANES : (c + 1) * LANES]
+                        * scale[j * z.heads : (j + 1) * z.heads]
+                    )
+            stats = jnp.where(lane_q == b, pair, stats)
+            stats = jnp.where(lane_q == z.seqs + b, t, stats)
+        return stats
+
+    stats = lax.fori_loop(0, z.seqs // 2, finish, jnp.zeros((z.queries, LANES), f32), unroll=4)
     turned = jnp.transpose(jnp.concatenate([stats, jnp.zeros((LANES - z.queries, LANES), f32)], axis=0))
     lane_s = lax.broadcasted_iota(jnp.int32, (z.seqs, LANES), 1)
     stat[...] = jnp.where(
@@ -344,7 +363,7 @@
             sendp[g, k] = jnp.concatenate(pieces, axis=0).astype(bf16)
             return carry
 
-        lax.fori_loop(0, z.chips, other_rows, 0, unroll=4)
+        lax.fori_loop(0, z.chips, other_rows, 0, unroll=16)
         sums_pair.append(pair_copy(2 + g, sendp.at[g], part.at[g]))
         sums_pair[g].start()
 
@@ -376,7 +395,7 @@
         send[k] = (yt[pl.ds((k * CORES + core) * z.head_stride, z.heads), :] + theirs).astype(bf16)
         return carry
 
-    lax.fori_loop(0, z.chips, own_rows, 0, unroll=4)
+    lax.fori_loop(0, z.chips, own_rows, 0, unroll=16)
 
     for i in order:
         sums_copy(i, chip).start()
@@ -440,11 +459,12 @@
         V((slots, latent, block), bf16),
         V((z.chunks * span, LANES), f32),
         V((z.seqs, z.queries, latent), bf16),
-        V((z.seqs, z.queries, LANES), f32),
+        V((z.seqs, z.queries, LANES), bf16),
         V((slots, z.queries, block), f32),
         V((slots, z.queries, block), f32),
         V((z.seqs, z.queries, block), f32),
-        V((z.seqs, z.queries, block), f32),
+        V((z.seqs // 2, z.queries, block), f32),
+        V((z.seqs // 2, z.queries, block), f32),
         V((slots, z.queries, block), f32),
         V((slots, z.queries, latent), f32),
         V((z.chunks * span, LANES), f32),

time: 28.6 us -> 27.8 us (0.972)
  Pallas kernels: 27 us -> 26.2 us
    pallas_call x1, Pallas kernels: 27 us -> 26.2 us  [per_device(): pl.pallas_call(functools.partial(kernel, z), out_shape=jax.ShapeDtypeStru...]
where the time goes in v6:
time: 27.8 us; the launch traced here: 27.5 us
  Pallas kernels  26.2 us (94%)
  local copies, waits for them, and re-layouts  1.34 us (5%)
    pallas_call x1, Pallas kernels, per_device(): pl.pallas_call(functools.partial(kernel, z), out_shape=jax.ShapeDtypeStru...  26.2 us
    unnamed x1, local copies, waits for them, and re-layouts  1.34 us

profile of v6, /device:TPU:1, one launch (start us, length us, event | category | flops | bytes accessed | tf_op | source)
XLA Modules:
  0.0 27.5 jit_solution(5474361809222694557)
XLA Ops:
  0.0 26.2 %shard_map.91 = bf16[1,4096]{1,0:T(2,128)(2,1)} custom-call(bf16[1,4096]{1,0:T(2,128)(2,1)} %qn_hbm.1, bf16[1,2048]{1,0:T(2,128)(2,1)} %qr_hbm.1, bf16[64,128,512]{2,1,0:T(8,128)(2,1)} %lat_hbm.1, bf16[64,8192]{1,0:T(8,128)(2,1)} %kr_hbm.1, bf16[32,128,512]{2,1,0:T(8,128)(2,1)} %ku_hbm.1, bf16[32,512,128]{2,1,0:T(8,128)(2,1)} %vu_hbm.1, s32[16]{0:T(128)} %len_hbm.1, ...), custom_call_target="tpu_custom_call" | custom-call | tf_op jit(solution)/shard_map/pallas_call | solution.py:488
  26.2 1.3 %copy.11 = bf16[1,4096]{1,0:T(2,128)(2,1)} copy(bf16[1,4096]{1,0:T(2,128)(2,1)} %shard_map.91) | data formatting | bytes 16384

commit v7 on v5

--- a/solution.py
+++ b/solution.py
@@ -42,7 +42,7 @@
     qn_hbm, qr_hbm, lat_hbm, kr_hbm, ku_hbm, vu_hbm, len_hbm, own_hbm, ownrow_hbm, num_hbm,
     out_ref,
     qn, qr, lat, kr, ku, vu, len_s, own_s, num_s, own_v, meta_v, meta_s,
-    gath, qstage, gathf, rk, kt, qlt, ql, qro, sc, mpre, mtop, mpart, lpre, opre, ot, yt,
+    gath, qown, qstage, gathf, rk, kt, qlt, ql, qro, sc, mpre, mtop, mpart, lpre, opre, ot, yt,
     sendp, part, send, recv, stat, statp, statf, statr, shares, acc, row_out,
     out_sem, load_sem, meta_sem, gs_sem, gr_sem, fs_sem, fr_sem, ps_sem, pr_sem, es_sem, er_sem, ss_sem, sr_sem,
 ):
@@ -82,9 +82,18 @@
         c.start()
 
     barrier = pltpu.get_barrier_semaphore()
-    for i in range(z.chips):
-        target = peer_chip(i) * CORES + core if i else partner
-        pl.semaphore_signal(barrier, inc=1, device_id={"ctx": target}, device_id_type=MESH)
+    hub = core == 1
+
+    def greet(device):
+        pl.semaphore_signal(barrier, inc=1, device_id={"ctx": device}, device_id_type=MESH)
+
+    def greet_all():
+        for k in range(z.chips):
+            greet(k * CORES)
+            pl.when(chip != k)(functools.partial(greet, k * CORES + 1))
+
+    pl.when(hub)(greet_all)
+    pl.when(jnp.logical_not(hub))(functools.partial(greet, partner))
 
     ld_qn.wait()
     ld_qr.wait()
@@ -92,43 +101,49 @@
         qstage[h : h + 1, :] = qn[:, h * LANES : (h + 1) * LANES].astype(f32)
     for h in range(z.pairs):
         qstage[z.heads + h : z.heads + h + 1, :] = qr[:, h * LANES : (h + 1) * LANES].astype(f32)
-    gath[core * z.chips + chip] = qstage[...].astype(bf16)
+    own_slot = core * z.chips + chip
+    qown[...] = qstage[...].astype(bf16)
+    gath[own_slot] = qown[...]
 
     pl.semaphore_wait(barrier, z.chips)
 
-    own_slot = core * z.chips + chip
-
-    def gather_copy(i):
-        return pltpu.make_async_remote_copy(
-            src_ref=gath.at[own_slot], dst_ref=gath.at[own_slot], send_sem=gs_sem, recv_sem=gr_sem,
-            device_id={"ctx": peer_chip(i) * CORES + core}, device_id_type=MESH,
-        )
-
-    def all_copies(src, dst, send_sem, recv_sem):
-        some = pl.ds(0, z.chips - 1)
+    def give(target):
+        pltpu.make_async_remote_copy(
+            src_ref=qown, dst_ref=gath.at[own_slot], send_sem=gs_sem, recv_sem=gr_sem.at[core],
+            device_id={"ctx": target * CORES + 1}, device_id_type=MESH,
+        ).start()
+
+    def all_copies(count, src, dst, send_sem, recv_sem):
+        some = pl.ds(0, count)
         return pltpu.make_async_remote_copy(
             src_ref=src.at[some], dst_ref=dst.at[some], send_sem=send_sem, recv_sem=recv_sem,
             device_id={"ctx": partner}, device_id_type=MESH,
         )
 
-    all_rows = all_copies(gath, gath, gs_sem, gr_sem)
-    half_rows = gath.at[pl.ds(core * z.chips, z.chips)]
-    forward = pltpu.make_async_remote_copy(
-        src_ref=half_rows, dst_ref=half_rows, send_sem=fs_sem, recv_sem=fr_sem,
-        device_id={"ctx": partner}, device_id_type=MESH,
-    )
+    rows_hub = all_copies(z.chips - 1, gath, gath, gs_sem, gr_sem.at[1])
+    rows_leaf = all_copies(z.chips, gath, gath, gs_sem, gr_sem.at[0])
+
+    def forward(kind):
+        half = gath.at[pl.ds(kind * z.chips, z.chips)]
+        return pltpu.make_async_remote_copy(
+            src_ref=half, dst_ref=half, send_sem=fs_sem.at[kind], recv_sem=fr_sem.at[kind],
+            device_id={"ctx": partner}, device_id_type=MESH,
+        )
 
     order = [i for i in far_first if i]
-    late_first = sorted(range(z.chips), key=lambda k: (-(k % side), k // side in (0, 1)))
-    for k in late_first:
-
-        def give():
-            pltpu.make_async_remote_copy(
-                src_ref=gath.at[own_slot], dst_ref=gath.at[own_slot], send_sem=gs_sem, recv_sem=gr_sem,
-                device_id={"ctx": k * CORES + core}, device_id_type=MESH,
-            ).start()
-
-        pl.when(chip != k)(give)
+
+    def early():
+        for k in sorted(range(z.chips), key=lambda k: (-(k % side), k // side in (0, 1))):
+            pl.when((chip != k) | (core == 0))(functools.partial(give, k))
+
+    def late():
+        for i in order:
+            give(peer_chip(i))
+        pl.when(core == 0)(functools.partial(give, chip))
+
+    is_late = chip_z >= side // 2
+    pl.when(is_late)(late)
+    pl.when(jnp.logical_not(is_late))(early)
 
     ld_ownv.wait()
     n = z.slots
@@ -161,17 +176,23 @@
         kt[p] = jnp.transpose(lat[p])
         return carry
 
-    for k in range(3):
+    for k in range(4):
         ld_lat[k].wait()
-        lax.fori_loop(k * piece, (k + 1) * piece, turn_keys, 0, unroll=2)
-
-    all_rows.wait_recv()
-    forward.start()
-
-    ld_lat[3].wait()
-    lax.fori_loop(3 * piece, 4 * piece, turn_keys, 0, unroll=2)
-
-    forward.wait_recv()
+        lax.fori_loop(k * piece, (k + 1) * piece, turn_keys, 0, unroll=4)
+
+    def hand_on():
+        rows_hub.wait_recv()
+        forward(1).start()
+        rows_leaf.wait_recv()
+        forward(0).start()
+
+    pl.when(hub)(hand_on)
+
+    def take():
+        forward(1).wait_recv()
+        forward(0).wait_recv()
+
+    pl.when(jnp.logical_not(hub))(take)
 
     for row in range(z.rows):
         gathf[pl.ds(row * z.gather_stride, z.block_rows), :] = gath[row % CORES * z.chips + row // CORES].astype(f32)
@@ -189,7 +210,7 @@
                 qlt[pl.ds(c * span + place, z.rows, stride=z.head_stride), :] = y[:, c * LANES : (c + 1) * LANES]
         return carry
 
-    lax.fori_loop(0, z.pairs, absorb, 0, unroll=8)
+    lax.fori_loop(0, z.pairs, absorb, 0, unroll=16)
 
     lane_p = lax.broadcasted_iota(jnp.int32, (z.pairs, LANES), 1)
 
@@ -202,9 +223,9 @@
                     pl.ds(start, z.heads), :
                 ].astype(bf16)
             both = gathf[pl.ds(r * z.gather_stride + z.heads, z.pairs), :]
-            qro[b, j * z.heads : j * z.heads + z.pairs, :] = jnp.where(lane_p < z.rope, both, 0.0)
+            qro[b, j * z.heads : j * z.heads + z.pairs, :] = jnp.where(lane_p < z.rope, both, 0.0).astype(bf16)
             other = pltpu.roll(both, z.rope, 1)
-            qro[b, j * z.heads + z.pairs : (j + 1) * z.heads, :] = jnp.where(lane_p < z.rope, other, 0.0)
+            qro[b, j * z.heads + z.pairs : (j + 1) * z.heads, :] = jnp.where(lane_p < z.rope, other, 0.0).astype(bf16)
         return carry
 
     lax.fori_loop(0, z.seqs, queries, 0, unroll=16)
@@ -226,7 +247,7 @@
         rhs = jnp.concatenate([kt[p] for p in ps], axis=1)
         full = jnp.dot(lhs, rhs, preferred_element_type=f32)
         lhs = jnp.concatenate([qro[b] for b in bs], axis=0)
-        rhs = jnp.concatenate([rk[p, 0 : z.block, :] for p in ps], axis=0)
+        rhs = jnp.concatenate([rk[p, 0 : z.block, :] for p in ps], axis=0).astype(bf16)
         full = full + lax.dot_general(lhs, rhs, contract_last, preferred_element_type=f32)
         for u in range(2):
             p, o, j = ps[u], os[u], js[u]
@@ -240,7 +261,7 @@
         return top, before
 
     lax.fori_loop(
-        0, n // 2, score, (jnp.full((z.queries, z.block), floor_value, f32), jnp.int32(-2)), unroll=8
+        0, n // 2, score, (jnp.full((z.queries, z.block), floor_value, f32), jnp.int32(-2)), unroll=32
     )
 
     lane_q = lax.broadcasted_iota(jnp.int32, (z.queries, LANES), 1)
@@ -283,7 +304,7 @@
         opre[j] = run
         return total, run, o
 
-    lax.fori_loop(0, n, weigh, (jnp.zeros((z.queries, z.block), f32), jnp.zeros((z.queries, z.latent), f32), jnp.int32(-2)), unroll=16)
+    lax.fori_loop(0, n, weigh, (jnp.zeros((z.queries, z.block), f32), jnp.zeros((z.queries, z.latent), f32), jnp.int32(-2)), unroll=64)
 
     top_copy.wait_recv()
 
@@ -344,7 +365,7 @@
             sendp[g, k] = jnp.concatenate(pieces, axis=0).astype(bf16)
             return carry
 
-        lax.fori_loop(0, z.chips, other_rows, 0, unroll=4)
+        lax.fori_loop(0, z.chips, other_rows, 0, unroll=16)
         sums_pair.append(pair_copy(2 + g, sendp.at[g], part.at[g]))
         sums_pair[g].start()
 
@@ -376,14 +397,14 @@
         send[k] = (yt[pl.ds((k * CORES + core) * z.head_stride, z.heads), :] + theirs).astype(bf16)
         return carry
 
-    lax.fori_loop(0, z.chips, own_rows, 0, unroll=4)
+    lax.fori_loop(0, z.chips, own_rows, 0, unroll=16)
 
     for i in order:
         sums_copy(i, chip).start()
     recv[chip] = send[chip]
 
-    all_stats = all_copies(statf, statr, ss_sem, sr_sem)
-    all_sums = all_copies(send, recv, es_sem, er_sem)
+    all_stats = all_copies(z.chips - 1, statf, statr, ss_sem, sr_sem)
+    all_sums = all_copies(z.chips - 1, send, recv, es_sem, er_sem)
     all_stats.wait_recv()
 
     s = jnp.concatenate([statr[d] for d in range(z.chips)], axis=0)
@@ -407,8 +428,13 @@
     out_copy = pltpu.make_async_copy(row_out, out_ref, out_sem)
     out_copy.start()
 
-    all_rows.wait_send()
-    forward.wait_send()
+    def sent_hub():
+        rows_hub.wait_send()
+        forward(0).wait_send()
+        forward(1).wait_send()
+
+    pl.when(hub)(sent_hub)
+    pl.when(jnp.logical_not(hub))(lambda: rows_leaf.wait_send())
     all_stats.wait_send()
     all_sums.wait_send()
     for c in (top_copy, stat_pair, *sums_pair):
@@ -434,13 +460,14 @@
         V(key_up.shape, bf16), V(value_up.shape, bf16), S(lengths.shape, jnp.int32), S(block_owner.shape, jnp.int32),
         S(block_number.shape, jnp.int32), V((1, slots), jnp.int32), V((8, LANES), jnp.int32), S((8, LANES), jnp.int32),
         V((z.rows, z.block_rows, LANES), bf16),
+        V((z.block_rows, LANES), bf16),
         V((z.block_rows, LANES), f32),
         V((z.rows * z.gather_stride, LANES), f32),
         V((slots, z.key_stride, LANES), f32),
         V((slots, latent, block), bf16),
         V((z.chunks * span, LANES), f32),
         V((z.seqs, z.queries, latent), bf16),
-        V((z.seqs, z.queries, LANES), f32),
+        V((z.seqs, z.queries, LANES), bf16),
         V((slots, z.queries, block), f32),
         V((slots, z.queries, block), f32),
         V((z.seqs, z.queries, block), f32),
@@ -461,7 +488,7 @@
         V((heads, z.value), f32),
         V((1, heads * z.value), bf16),
         D,
-        D((13,)), D, D, D, D, D,
+        D((13,)), D, D, D((2,)), D((2,)), D((2,)),
         D((4,)), D((4,)),
         D, D, D, D,
     ]

time: 28.6 us -> 27 us (0.944)
  Pallas kernels: 27 us -> 25.4 us
    pallas_call x1, Pallas kernels: 27 us -> 25.4 us  [per_device(): pl.pallas_call(functools.partial(kernel, z), out_shape=jax.ShapeDtypeStru...]
where the time goes in v7:
time: 27 us; the launch traced here: 26.7 us
  Pallas kernels  25.4 us (94%)
  local copies, waits for them, and re-layouts  1.34 us (5%)
    pallas_call x1, Pallas kernels, per_device(): pl.pallas_call(functools.partial(kernel, z), out_shape=jax.ShapeDtypeStru...  25.4 us
    unnamed x1, local copies, waits for them, and re-layouts  1.34 us

profile of v7, /device:TPU:1, one launch (start us, length us, event | category | flops | bytes accessed | tf_op | source)
XLA Modules:
  0.0 26.7 jit_solution(764349836367028164)
XLA Ops:
  0.0 25.4 %shard_map.91 = bf16[1,4096]{1,0:T(2,128)(2,1)} custom-call(bf16[1,4096]{1,0:T(2,128)(2,1)} %qn_hbm.1, bf16[1,2048]{1,0:T(2,128)(2,1)} %qr_hbm.1, bf16[64,128,512]{2,1,0:T(8,128)(2,1)} %lat_hbm.1, bf16[64,8192]{1,0:T(8,128)(2,1)} %kr_hbm.1, bf16[32,128,512]{2,1,0:T(8,128)(2,1)} %ku_hbm.1, bf16[32,512,128]{2,1,0:T(8,128)(2,1)} %vu_hbm.1, s32[16]{0:T(128)} %len_hbm.1, ...), custom_call_target="tpu_custom_call" | custom-call | tf_op jit(solution)/shard_map/pallas_call | solution.py:495
  25.4 1.3 %copy.11 = bf16[1,4096]{1,0:T(2,128)(2,1)} copy(bf16[1,4096]{1,0:T(2,128)(2,1)} %shard_map.91) | data formatting | bytes 16384

commit v8 on v7

--- a/solution.py
+++ b/solution.py
@@ -78,8 +78,6 @@
         )
     ]
     ld_qn, ld_qr, ld_ownv, ld_len, ld_own, ld_num, ld_kr, *ld_lat, ld_ku, ld_vu = loads
-    for c in loads:
-        c.start()
 
     barrier = pltpu.get_barrier_semaphore()
     hub = core == 1
@@ -94,6 +92,8 @@
 
     pl.when(hub)(greet_all)
     pl.when(jnp.logical_not(hub))(functools.partial(greet, partner))
+    for c in loads:
+        c.start()
 
     ld_qn.wait()
     ld_qr.wait()

time: 27 us -> 27 us (level)
  no operation moved by 1% of the time
where the time goes in v8:
time: 27 us; the launch traced here: 26.7 us
  Pallas kernels  25.4 us (94%)
  local copies, waits for them, and re-layouts  1.34 us (5%)
    pallas_call x1, Pallas kernels, per_device(): pl.pallas_call(functools.partial(kernel, z), out_shape=jax.ShapeDtypeStru...  25.4 us
    unnamed x1, local copies, waits for them, and re-layouts  1.34 us

profile of v8, /device:TPU:1, one launch (start us, length us, event | category | flops | bytes accessed | tf_op | source)
XLA Modules:
  0.0 26.7 jit_solution(9756022664778884485)
XLA Ops:
  0.0 25.4 %shard_map.91 = bf16[1,4096]{1,0:T(2,128)(2,1)} custom-call(bf16[1,4096]{1,0:T(2,128)(2,1)} %qn_hbm.1, bf16[1,2048]{1,0:T(2,128)(2,1)} %qr_hbm.1, bf16[64,128,512]{2,1,0:T(8,128)(2,1)} %lat_hbm.1, bf16[64,8192]{1,0:T(8,128)(2,1)} %kr_hbm.1, bf16[32,128,512]{2,1,0:T(8,128)(2,1)} %ku_hbm.1, bf16[32,512,128]{2,1,0:T(8,128)(2,1)} %vu_hbm.1, s32[16]{0:T(128)} %len_hbm.1, ...), custom_call_target="tpu_custom_call" | custom-call | tf_op jit(solution)/shard_map/pallas_call | solution.py:495
  25.4 1.3 %copy.11 = bf16[1,4096]{1,0:T(2,128)(2,1)} copy(bf16[1,4096]{1,0:T(2,128)(2,1)} %shard_map.91) | data formatting | bytes 16384
